TPU v7x, 32 devices: a whole 2x2x4 slice. The times are simulated.
32 devices in a mesh: dp: 4 (over y, x), land: 8 (over z, core).
Axes of the slice: x: 2, y: 2, z: 4, core: 2. Of those that a mesh axis runs over, the one named last changes fastest.
Arguments:
- items: bfloat16 [16384, 768], P(('dp', 'land')), may hold values from -1.5 to 1.5
- landmarks: bfloat16 [8192, 768], P('land'), may hold values from -1.5 to 1.5
- scales: float32 [8192], P('land'), may hold values from 0.25 to 1
- eigvecs: bfloat16 [8192, 256], P('land'), may hold values from -0.0625 to 0.0625
- eigvals: float32 [256], replicated, may hold values from 0.5 to 2
Outputs:
- coords: float32 [16384, 256], P(('dp', 'land'))
- gram: float32 [256, 256], replicated
All inputs are finite; a program needn't handle non-finite values.
Results may differ from a plain program's by a relative error of at most 0.0028.
Values may be sent and summed in bfloat16 or wider, within the bound.
No kernel may reach another device: no remote copies, remote signals or barrier semaphores. Data moves between devices by JAX's collectives and lax.ppermute only.
A program may use at most 128 MiB of HBM per device.

v0:
```python
import jax
import jax.numpy as jnp
from jax import lax
from jax.sharding import PartitionSpec as P


def kernel_block(rows, landmarks, scales):
    row_vals = rows.astype(jnp.float32)
    land_vals = landmarks.astype(jnp.float32)
    row_sq = jnp.sum(row_vals * row_vals, axis=1)
    land_sq = jnp.sum(land_vals * land_vals, axis=1)
    cross = jnp.dot(rows, landmarks.T, preferred_element_type=jnp.float32)
    dist = row_sq[:, None] + land_sq[None, :] - 2.0 * cross
    return jnp.exp(-dist * scales[None, :])


def per_device(items, landmarks, scales, eigvecs, eigvals):
    own_rows = items.shape[0]
    rows_all = own_rows * lax.axis_size("dp") * lax.axis_size("land")
    landmark_count = landmarks.shape[0] * lax.axis_size("land")
    kernel = kernel_block(lax.all_gather(items, "land", axis=0, tiled=True), landmarks, scales)
    land_degree = lax.psum(jnp.sum(kernel, axis=0), "dp")
    row_part = jnp.sum(kernel, axis=1)
    scaled = (kernel / jnp.sqrt(land_degree)[None, :]).astype(jnp.bfloat16)
    partial_value = jnp.dot(scaled, eigvecs, preferred_element_type=jnp.float32)
    summed, degrees = (
        lax.psum_scatter(partial_value, "land", scatter_dimension=0, tiled=True),
        lax.psum_scatter(row_part, "land", scatter_dimension=0, tiled=True),
    )
    factor = jnp.sqrt(jnp.float32(rows_all) * jnp.float32(landmark_count))
    coords = summed * (factor / jnp.sqrt(degrees))[:, None] / eigvals[None, :]
    outer = jnp.dot(coords.T, coords, precision=lax.Precision.HIGHEST)
    gram = lax.psum(outer, ("dp", "land")) / jnp.float32(rows_all)
    return (coords, gram)


def solution(mesh):
    return jax.shard_map(
        per_device,
        mesh=mesh,
        in_specs=(P(("dp", "land"), None), P("land", None), P("land"), P("land", None), P()),
        out_specs=(P(("dp", "land"), None), P()),
        check_vma=False,
    )
```

profile of v0, /device:TPU:0, one launch (start us, length us, event | category | flops | bytes accessed | tf_op | source)
XLA Modules:
  0.0 303.2 jit_solution(13520838185477166311)
XLA Ops:
  7.2 0.0 copy-start
  7.2 0.0 all-gather.2.cloned.1.call-start
  7.2 0.7 all-gather.2.cloned.1.call-update
  7.9 0.0 reduce-scatter.2.cloned.1.call-start
  8.0 1.8 multiply_reduce_fusion.1
  9.7 67.3 %all-gather.2.cloned.1.call-done = bf16[4096,768]{1,0:T(8,128)(2,1)} async-done(((bf16[512,768]{1,0:T(8,128)(2,1)}), bf16[4096,768]{1,0:T(8,128)(2,1)}) %all-gather.2.cloned.1.call-update) | async-done | bytes 6291472 | tf_op jit(solution)/shard_map/all_gather | solution.py:21
  77.1 4.1 %multiply_reduce_fusion = f32[4096]{0:T(1024)S(1)} fusion(bf16[4096,768]{1,0:T(8,128)(2,1)} %all-gather.2.cloned.1.call-done), kind=kLoop, calls=%fused_computation.2 | loop fusion | flops 9433088 | bytes 6307840 | tf_op jit(solution)/shard_map/reduce_sum | solution.py:10
  81.2 15.5 %fusion.2 = (f32[4096]{0:T(1024)S(1)}, f32[1024]{0:T(1024)S(1)}, f32[4096,1024]{1,0:T(8,128)}) fusion(f32[1024]{0:T(1024)} %param.7, bf16[4096,768]{1,0:T(8,128)(2,1)} %all-gather.2.cloned.1.call-done, bf16[1024,768]{1,0:T(8,128)(2,1)} %param.6, f32[1024]{0:T(1024)S(1)} %multiply_reduce_fusion.1, f32[4096]{0:T(1024)S(1)} %multiply_reduce_fusion), kind=kOutput, calls=%fused_computation.9 | convolution fusion | flops 6471805952 | bytes 24686592 | tf_op jit(solution)/shard_map/dot_general | solution.py:12
  96.6 9.8 %psum.14 = f32[1024]{0:T(1024)S(1)} all-reduce(f32[1024]{0:T(1024)S(1)} %get-tuple-element.3), channel_id=1, replica_groups=mesh['dp'=4,'land'=8] {'dp'}, use_global_device_ids=true, to_apply=%region_3.0 | all-reduce | flops 1024 | bytes 8192 | tf_op jit(solution)/shard_map/psum | solution.py:22
  106.5 0.0 copy-start.3
  106.5 0.0 copy-start.2
  106.5 10.1 %fusion = f32[4096,256]{1,0:T(8,128)} fusion(bf16[1024,256]{1,0:T(8,128)(2,1)S(1)} %copy-done, f32[4096,1024]{1,0:T(8,128)} %get-tuple-element.4, f32[1024]{0:T(1024)S(1)} %sqrt.6), kind=kOutput, calls=%fused_computation.3 | convolution fusion | flops 2155872256 | bytes 21499904 | tf_op jit(solution)/shard_map/dot_general | solution.py:25
  116.5 0.0 reduce-scatter.2.cloned.1.call-update
  116.6 0.0 all-reduce.3.cloned.1.call-start
  116.6 0.6 dynamic-slice
  117.9 27.3 %all-reduce = f32[4096]{0:T(1024)S(1)} all-reduce(f32[4096]{0:T(1024)S(1)} %get-tuple-element.2), channel_id=3, replica_groups=mesh['dp'=4,'land'=8] {'land'}, use_global_device_ids=true, to_apply=%region_6.0.clone | all-reduce | flops 4096 | bytes 32768
  145.1 0.1 fusion.1
  145.2 18.9 %reduce-scatter.2.cloned.1.call-done = f32[512,256]{1,0:T(8,128)} async-done(((f32[4096,256]{1,0:T(8,128)}), f32[512,256]{1,0:T(8,128)}) %reduce-scatter.2.cloned.1.call-update) | async-done | bytes 524304 | tf_op jit(solution)/shard_map/reduce_scatter | solution.py:27
  164.0 1.2 multiply_divide_fusion
  165.2 0.0 copy-start.1
  165.2 1.7 fusion.3
  167.0 0.0 all-reduce.3.cloned.1.call-update
  167.0 127.9 %all-reduce.3.cloned.1.call-done = f32[256,256]{1,0:T(8,128)} async-done(((f32[256,256]{1,0:T(8,128)}), f32[256,256]{1,0:T(8,128)}) %all-reduce.3.cloned.1.call-update) | async-done | bytes 262160 | tf_op jit(solution)/shard_map/psum | solution.py:33
  295.0 1.7 broadcast_multiply_fusion
  (5 shorter events, 0.0 us)
Async XLA Ops:
  7.2 99.3 %copy-start = (bf16[1024,256]{1,0:T(8,128)(2,1)S(1)}, bf16[1024,256]{1,0:T(8,128)(2,1)}, u32[]{:S(2)}) copy-start(bf16[1024,256]{1,0:T(8,128)(2,1)} %param.8) | copy-start | bytes 1572868
  7.2 69.9 %all-gather.2.cloned.1.call-start = ((), (), s32[]{:S(2)}) async-start(), calls=%async_computation.1 | async-start | bytes 7077888 | tf_op jit(solution)/shard_map/all_gather | solution.py:21
  7.9 156.1 %reduce-scatter.2.cloned.1.call-start = ((), (), s32[]{:S(2)}) async-start(), calls=%async_computation.2 | async-start | bytes 4718592 | tf_op jit(solution)/shard_map/reduce_scatter | solution.py:27
  106.5 10.2 %copy-start.3 = (u32[32]{0:T(128)S(1)}, u32[32]{0:T(128)}, u32[]{:S(2)}) copy-start(u32[32]{0:T(128)} %constant.11) | copy-start | bytes 388
  106.5 57.6 %copy-start.2 = (f32[256]{0:T(256)S(1)}, f32[256]{0:T(256)}, u32[]{:S(2)}) copy-start(f32[256]{0:T(256)} %param.9) | copy-start | bytes 3076
  116.6 178.4 %all-reduce.3.cloned.1.call-start = ((), (), s32[]{:S(2)}) async-start(), calls=%async_computation.3 | async-start | bytes 524288 | tf_op jit(solution)/shard_map/psum | solution.py:33
  165.2 131.4 %copy-start.1 = (f32[512,256]{1,0:T(8,128)}, f32[512,256]{1,0:T(8,128)S(1)}, u32[]{:S(2)}) copy-start(f32[512,256]{1,0:T(8,128)S(1)} %multiply_divide_fusion) | copy-start | bytes 1572868
Sparse Core Ops, SparseCore 0:
  9.6 67.4 all-gather.1
  116.7 47.3 reduce-scatter.1
  170.1 124.7 all-reduce.2
where the time goes:
time: 303 us
  waiting for transfers between devices  215 us (71%)
  blocking collectives  37.1 us (12%)
  matrix products  27.3 us (9%)
  between operations  14.5 us (5%)
  other arithmetic  8.79 us (3%)
    psum x1, waiting for transfers between devices, per_device(): gram = lax.psum(outer, ('dp', 'land')) / jnp.float32(rows_all)  128 us
    all_gather x1, waiting for transfers between devices, per_device(): lax.all_gather(items, 'land', axis=0, tiled=True)  67.3 us
    unnamed x1, blocking collectives  27.3 us
    reduce_scatter x1, waiting for transfers between devices, per_device(): lax.psum_scatter(partial_value, 'land', scatter_dimension=0, tiled=True)  18.9 us
    dot_general x1, matrix products, kernel_block(): cross = jnp.dot(rows, landmarks.T, preferred_element_type=jnp.float32)  15.5 us
    dot_general x1, matrix products, per_device(): partial_value = jnp.dot(scaled, eigvecs, preferred_element_type=jnp.float32)  10.1 us
    psum x1, blocking collectives, per_device(): land_degree = lax.psum(jnp.sum(kernel, axis=0), 'dp')  9.82 us
  transfers between devices with their start and end apart: 3, of which 3 were waited for; matrix products, arithmetic and copies ran while one was open for 1% of the time, Pallas kernels for 0%

commit v1 on v0

v1 whole, which is shorter than its diff:
```python
import functools
import math

import jax
import jax.numpy as jnp
from jax import lax
from jax.experimental import pallas as pl
from jax.experimental.pallas import tpu as pltpu
from jax.sharding import PartitionSpec as P

F32 = jnp.float32
B16 = jnp.bfloat16
EXTRA = 16
VMEM = pl.BlockSpec(memory_space=pltpu.VMEM)
SMEM = pl.BlockSpec(memory_space=pltpu.SMEM)
TRANS = (((1,), (1,)), ((), ()))


def split3(x):
    hi = x.astype(B16)
    rest = x - hi.astype(F32)
    mid = rest.astype(B16)
    return hi, mid, (rest - mid.astype(F32)).astype(B16)


def prep_body(pos_ref, land_ref, scale_ref, vec_ref, msg_ref, vmsg_ref):
    stripe, depth = land_ref.shape
    msg_ref[stripe:, :] = jnp.zeros((EXTRA, depth), B16)
    land = land_ref[...]
    msg_ref[:stripe, :] = land
    vmsg_ref[...] = vec_ref[...]
    vals = land.astype(F32)
    squares = vals * vals
    high = squares.astype(B16)
    low = (squares - high.astype(F32)).astype(B16)
    ones = jnp.ones((8, depth), B16)
    norm = lax.dot_general(ones, high, TRANS, preferred_element_type=F32)
    norm = norm + lax.dot_general(ones, low, TRANS, preferred_element_type=F32)
    rows = split3(scale_ref[0]) + split3(norm[:1])
    block = jnp.concatenate([r.astype(F32) for r in rows] + [jnp.zeros((EXTRA - 6, stripe), F32)], axis=0)
    msg_ref[stripe:, :stripe] = block.astype(B16)


def prep(pos, landmarks, scales, eigvecs, parts):
    count, depth = landmarks.shape
    stripe = count // parts
    width = eigvecs.shape[1]
    return pl.pallas_call(
        prep_body,
        grid_spec=pltpu.PrefetchScalarGridSpec(
            num_scalar_prefetch=1,
            grid=(1,),
            in_specs=[
                pl.BlockSpec((stripe, depth), lambda i, p: (p[0], 0)),
                pl.BlockSpec((1, 1, stripe), lambda i, p: (p[0], 0, 0)),
                pl.BlockSpec((stripe, width), lambda i, p: (p[0], 0)),
            ],
            out_specs=[
                pl.BlockSpec((stripe + EXTRA, depth), lambda i, p: (0, 0)),
                pl.BlockSpec((stripe, width), lambda i, p: (0, 0)),
            ],
        ),
        out_shape=[
            jax.ShapeDtypeStruct((stripe + EXTRA, depth), B16),
            jax.ShapeDtypeStruct((stripe, width), B16),
        ],
        name="prep",
    )(pos, landmarks, scales.reshape(parts, 1, stripe), eigvecs)


def block_body(*refs, groups, slot, chunk, first_col):
    nrow = sum(groups)
    rows = refs[:nrow]
    msgs = refs[nrow : nrow + 2]
    col_in = refs[nrow + 2]
    row_in = refs[nrow + 3 : nrow + 3 + len(groups)]
    outs = refs[nrow + 3 + len(groups) :]
    kern = outs[: len(groups)]
    col_out = outs[len(groups)]
    row_out = outs[len(groups) + 1 :]
    stripe = msgs[0].shape[0] - EXTRA
    log2e = math.log2(math.e)

    def triple(ref, at):
        part = ref[stripe:, :stripe].astype(F32)
        return part[at : at + 1] + part[at + 1 : at + 2] + part[at + 2 : at + 3]

    neg = [triple(m, 0) * (-log2e) for m in msgs]
    norm = [triple(m, 3) for m in msgs]
    cols = [jnp.zeros((8, stripe), F32) for _ in msgs]
    at = 0
    for g, pieces in enumerate(groups):
        base = 0
        for piece in range(pieces):
            src = rows[at]
            at += 1

            def step(i, carry, src=src, g=g, base=base):
                start = pl.multiple_of(i * chunk, chunk)
                block = src[pl.ds(start, chunk), :]
                vals = block.astype(F32)
                sq = jnp.sum(vals * vals, axis=1, keepdims=True)
                fresh = []
                lanes = jnp.zeros((chunk, 128), F32)
                for e, m in enumerate(msgs):
                    cross = lax.dot_general(block, m[:stripe, :], TRANS, preferred_element_type=F32)
                    dist = (sq + norm[e]) - 2.0 * cross
                    value = jnp.exp2(dist * neg[e])
                    kern[g][pl.ds(base + start, chunk), e * stripe : (e + 1) * stripe] = value
                    fresh.append(carry[e] + jnp.sum(value.reshape(chunk // 8, 8, stripe), axis=0))
                    for q in range(stripe // 128):
                        lanes = lanes + value[:, q * 128 : (q + 1) * 128]
                for q in range(chunk // 128):
                    row = jnp.sum(lanes[q * 128 : (q + 1) * 128].T, axis=0, keepdims=True)
                    spot = pl.ds(pl.multiple_of(base + start + q * 128, 128), 128)
                    row_out[g][:, spot] = row_in[g][:, spot] + row
                return tuple(fresh)

            cols = list(lax.fori_loop(0, src.shape[0] // chunk, step, tuple(cols)))
            base += src.shape[0]
    total = jnp.concatenate([jnp.sum(c, axis=0, keepdims=True) for c in cols], axis=1)
    if first_col:
        col_out[...] = total
    else:
        col_out[...] = col_in[...] + total


def block_call(row_groups, msgs, col_in, row_in, name):
    groups = tuple(len(g) for g in row_groups)
    flat = [r for g in row_groups for r in g]
    depth = flat[0].shape[1]
    stripe = msgs[0].shape[0] - EXTRA
    sizes = [sum(r.shape[0] for r in g) for g in row_groups]
    chunk = min(256, min(r.shape[0] for r in flat))
    out_shape = (
        [jax.ShapeDtypeStruct((n, 2 * stripe), F32) for n in sizes]
        + [jax.ShapeDtypeStruct((1, 2 * stripe), F32)]
        + [jax.ShapeDtypeStruct((1, n), F32) for n in sizes]
    )
    flops = 2 * sum(sizes) * 2 * stripe * depth
    outs = pl.pallas_call(
        functools.partial(block_body, groups=groups, slot=0, chunk=chunk, first_col=False),
        out_shape=out_shape,
        in_specs=[VMEM] * (len(flat) + 2 + 1 + len(groups)),
        out_specs=[VMEM] * len(out_shape),
        cost_estimate=pl.CostEstimate(flops=flops, bytes_accessed=0, transcendentals=sum(sizes) * 2 * stripe),
        compiler_params=pltpu.CompilerParams(vmem_limit_bytes=24 << 20),
        name=name,
    )(*flat, *msgs, col_in, *row_in)
    n = len(groups)
    return outs[:n], outs[n], outs[n + 1 :]


def apply_body(*refs, slots, peers):
    kern = refs[:slots]
    vecs = refs[slots : 3 * slots]
    degs = refs[3 * slots : 3 * slots + 1 + peers]
    out = refs[-1]
    stripe = vecs[0].shape[0]
    acc = None
    for k in range(slots):
        total = degs[0][k : k + 1, :]
        for j in range(1, peers + 1):
            total = total + degs[j][k ^ j : (k ^ j) + 1, :]
        weight = lax.rsqrt(total)
        for e in range(2):
            span = slice(e * stripe, (e + 1) * stripe)
            scaled = (kern[k][:, span] * weight[:, span]).astype(B16)
            term = jnp.dot(scaled, vecs[2 * k + e][...], preferred_element_type=F32)
            acc = term if acc is None else acc + term
    out[...] = acc.astype(out.dtype)


def apply_call(kern, vecs, degs, dtype, name):
    rows = kern[0].shape[0]
    width = vecs[0].shape[1]
    flops = 2 * rows * width * sum(v.shape[0] for v in vecs)
    return pl.pallas_call(
        functools.partial(apply_body, slots=len(kern), peers=len(degs) - 1),
        out_shape=jax.ShapeDtypeStruct((rows, width), dtype),
        in_specs=[VMEM] * (len(kern) + len(vecs) + len(degs)),
        out_specs=VMEM,
        cost_estimate=pl.CostEstimate(flops=flops, bytes_accessed=0, transcendentals=0),
        compiler_params=pltpu.CompilerParams(vmem_limit_bytes=24 << 20),
        name=name,
    )(*kern, *vecs, *degs)


def finish_body(core_ref, *refs, parts, factor):
    sums = refs[:parts]
    degs = refs[parts : 2 * parts]
    eig_ref = refs[2 * parts]
    coords_ref, keep_ref, send_ref = refs[2 * parts + 1 :]
    rows, width = coords_ref.shape
    half = width // 2
    deg = degs[0][...]
    for d in degs[1:]:
        deg = deg + d[...]
    gain = factor / jnp.sqrt(deg)
    inv = 1.0 / eig_ref[...]
    highs, lows = [], []
    for q in range(rows // 128):
        span = slice(q * 128, (q + 1) * 128)
        column = jnp.broadcast_to(gain[:, span], (128, 128)).T
        total = sums[0][span, :].astype(F32)
        for s in sums[1:]:
            total = total + s[span, :].astype(F32)
        value = jnp.concatenate(
            [total[:, k * 128 : (k + 1) * 128] * column for k in range(width // 128)], axis=1
        ) * inv
        coords_ref[span, :] = value
        high = value.astype(B16)
        highs.append(high)
        lows.append((value - high.astype(F32)).astype(B16))
    high = jnp.concatenate(highs, axis=0)
    low = jnp.concatenate(lows, axis=0)
    dims = (((0,), (0,)), ((), ()))
    outer = lax.dot_general(high, high, dims, preferred_element_type=F32)
    outer = outer + lax.dot_general(high, low, dims, preferred_element_type=F32)
    outer = outer + lax.dot_general(low, high, dims, preferred_element_type=F32)
    first = core_ref[0] == 0
    top, bottom = outer[:half], outer[half:]
    keep_ref[...] = jnp.where(first, top, bottom)
    send_ref[...] = jnp.where(first, bottom, top).astype(B16)


def finish_call(core, sums, degs, eigvals, factor):
    rows, width = sums[0].shape
    return pl.pallas_call(
        functools.partial(finish_body, parts=len(sums), factor=factor),
        out_shape=[
            jax.ShapeDtypeStruct((rows, width), F32),
            jax.ShapeDtypeStruct((width // 2, width), F32),
            jax.ShapeDtypeStruct((width // 2, width), B16),
        ],
        in_specs=[SMEM] + [VMEM] * (2 * len(sums) + 1),
        out_specs=[VMEM] * 3,
        compiler_params=pltpu.CompilerParams(vmem_limit_bytes=24 << 20),
        name="finish",
    )(core, *sums, *degs, eigvals.reshape(1, width))


def exchange(x, axis, offset):
    size = lax.axis_size(axis)
    return lax.ppermute(x, axis, [(i, i ^ offset) for i in range(size)])


def gather_rows(x, size):
    if size != 4:
        return [[x]] + [[exchange(x, "dp", d)] for d in range(1, size)]
    half = x.shape[0] // 2
    one = exchange(x, "dp", 1)
    two = exchange(x, "dp", 2)
    return [[x], [one], [two], [exchange(one[:half], "dp", 2), exchange(two[half:], "dp", 1)]]


def gather_chips(x, chips):
    if chips != 4:
        return [x] + [exchange(x, "land", 2 * k) for k in range(1, chips)]
    two = exchange(x, "land", 4)
    one = exchange(x, "land", 2)
    inner = lax.ppermute(x, "land", [(2, 4), (3, 5), (4, 2), (5, 3)])
    outer = lax.ppermute(two, "land", [(4, 6), (5, 7), (2, 0), (3, 1)])
    edge = lax.axis_index("land") // 2
    three = jnp.where((edge == 0) | (edge == chips - 1), outer, inner)
    return [x, one, two, three]


def per_device(items, landmarks, scales, eigvecs, eigvals):
    dp = lax.axis_size("dp")
    land = lax.axis_size("land")
    chips = land // 2
    own = items.shape[0]
    width = eigvecs.shape[1]
    rows_all = own * dp * land
    landmark_count = landmarks.shape[0] * land
    pos = lax.axis_index("dp").astype(jnp.int32).reshape(1)
    core = (lax.axis_index("land") % 2).astype(jnp.int32).reshape(1)

    msg, vmsg = prep(pos, landmarks, scales, eigvecs, dp)
    stripe = vmsg.shape[0]
    row_sets = gather_rows(items, dp)
    mine = gather_chips(msg, chips)
    mates = [exchange(m, "land", 1) for m in mine]
    vmsg, _ = lax.optimization_barrier((vmsg, mine[-1]))
    vmine = gather_chips(vmsg, chips)
    vmates = [exchange(m, "land", 1) for m in vmine]

    kern = [[None] * chips for _ in range(dp)]
    col = [jnp.zeros((1, 2 * stripe), F32) for _ in range(chips)]
    row = [jnp.zeros((1, own), F32) for _ in range(dp)]
    plan = [[0]] + ([[1, 2], [3]] if dp == 4 else [[d] for d in range(1, dp)])
    for group in plan:
        for k in range(chips):
            sets = [row_sets[d] for d in group]
            out, col[k], rows_out = block_call(sets, (mine[k], mates[k]), col[k], [row[d] for d in group], f"block{group[0]}_{k}")
            for i, d in enumerate(group):
                kern[d][k] = out[i]
                row[d] = rows_out[i]

    deg = jnp.concatenate(col, axis=0)
    mate = exchange(deg, "land", 1)
    deg = deg + jnp.concatenate([mate[:, stripe:], mate[:, :stripe]], axis=1)
    degs = [deg] + [exchange(deg, "land", 2 * k) for k in range(1, chips)]
    row_deg = [row[0]] + [exchange(row[d], "dp", d) for d in range(1, dp)]
    vecs = [v for pair in zip(vmine, vmates) for v in pair]

    sums = [None] * dp
    for d in list(range(dp - 1, 0, -1)) + [0]:
        part = apply_call(kern[d], vecs, degs, B16 if d else F32, f"apply{d}")
        sums[d] = exchange(part, "dp", d) if d else part

    factor = math.sqrt(float(rows_all) * float(landmark_count))
    coords, keep, send = finish_call(core, sums, row_deg, eigvals, factor)
    total = keep + exchange(send, "land", 1).astype(F32)
    for axis, size in (("dp", dp), ("land", land)):
        step = 1 if axis == "dp" else 2
        while step < size:
            total = lax.reduce_precision(total, 8, 7)
            total = total + exchange(total.astype(B16), axis, step).astype(F32)
            step *= 2
    total = total * (1.0 / rows_all)
    other = exchange(total, "land", 1)
    first = (core == 0).reshape(1, 1)
    gram = jnp.concatenate([jnp.where(first, total, other), jnp.where(first, other, total)], axis=0)
    return (coords, gram)


def solution(mesh):
    return jax.shard_map(
        per_device,
        mesh=mesh,
        in_specs=(P(("dp", "land"), None), P("land", None), P("land"), P("land", None), P()),
        out_specs=(P(("dp", "land"), None), P()),
        check_vma=False,
    )
```

time: 303 us -> 128 us (0.42)
  waiting for transfers between devices: 215 us -> 47.2 us
  starting transfers between devices: 0.12 us -> 38.3 us
  blocking collectives: 37.1 us -> 0 us
  Pallas kernels: 0 us -> 28.8 us
  matrix products: 27.3 us -> 0 us
  between operations: 14.5 us -> 1.01 us
  local copies, waits for them, and re-layouts: 0.62 us -> 10.6 us
  other arithmetic: 8.79 us -> 1.99 us
    psum x1 -> x0, waiting for transfers between devices: 128 us -> none  [per_device(): gram = lax.psum(outer, ('dp', 'land')) / jnp.float32(rows_all)]
    all_gather x1 -> x0, waiting for transfers between devices: 67.3 us -> none  [per_device(): lax.all_gather(items, 'land', axis=0, tiled=True)]
    ppermute x0 -> x36, waiting for transfers between devices: none -> 47.2 us  [the longest x32 42 us: exchange(): return lax.ppermute(x, axis, [(i, i ^ offset) for i in range(size)])]
    ppermute x0 -> x36, starting transfers between devices: none -> 38.3 us  [the longest x32 33.4 us: exchange(): return lax.ppermute(x, axis, [(i, i ^ offset) for i in range(size)])]
    pallas_call x0 -> x18, Pallas kernels: none -> 28.8 us  [the longest x12 20.6 us: block_call(): pl.pallas_call(functools.partial(block_body, groups=groups, slot=0, chunk...]
    dot_general x3 -> x0, matrix products: 27.3 us -> none  [the longest x1 15.5 us: kernel_block(): cross = jnp.dot(rows, landmarks.T, preferred_element_type=jnp.float32)]
    unnamed x1 -> x0, blocking collectives: 27.3 us -> none
    reduce_scatter x1 -> x0, waiting for transfers between devices: 18.9 us -> none  [per_device(): lax.psum_scatter(partial_value, 'land', scatter_dimension=0, tiled=True)]
  transfers between devices with their start and end apart: 3 -> 36, of which waited for: 3 -> 13; matrix products, arithmetic and copies ran while one was open for 1% -> 2% of each run, Pallas kernels for 0% -> 19%
where the time goes in v1:
time: 128 us
  waiting for transfers between devices  47.2 us (37%)
  starting transfers between devices  38.3 us (30%)
  Pallas kernels  28.8 us (22%)
  local copies, waits for them, and re-layouts  10.6 us (8%)
  other arithmetic  1.99 us (2%)
    ppermute x32, waiting for transfers between devices, exchange(): return lax.ppermute(x, axis, [(i, i ^ offset) for i in range(size)])  42 us
    ppermute x32, starting transfers between devices, exchange(): return lax.ppermute(x, axis, [(i, i ^ offset) for i in range(size)])  33.4 us
    pallas_call x12, Pallas kernels, block_call(): pl.pallas_call(functools.partial(block_body, groups=groups, slot=0, chunk...  20.6 us
    unnamed x28, local copies, waits for them, and re-layouts  8.56 us
    ppermute x2, waiting for transfers between devices, gather_chips(): outer = lax.ppermute(two, 'land', [(4, 6), (5, 7), (2, 0), (3, 1)])  5.16 us
    pallas_call x4, Pallas kernels, apply_call(): pl.pallas_call(functools.partial(apply_body, slots=len(kern), peers=len(d...  5 us
    ppermute x2, starting transfers between devices, gather_chips(): outer = lax.ppermute(two, 'land', [(4, 6), (5, 7), (2, 0), (3, 1)])  2.75 us
  transfers between devices with their start and end apart: 36, of which 13 were waited for; matrix products, arithmetic and copies ran while one was open for 2% of the time, Pallas kernels for 19%

profile of v1, /device:TPU:0, one launch (start us, length us, event | category | flops | bytes accessed | tf_op | source)
XLA Modules:
  0.0 127.8 jit_solution(12746372098466879442)
XLA Ops:
  0.6 2.2 %prep.1 = (bf16[272,768]{1,0:T(8,128)(2,1)}, bf16[256,256]{1,0:T(8,128)(2,1)}) custom-call(s32[1]{0:T(128)} %bitcast.1.pos_ref, bf16[1024,768]{1,0:T(8,128)(2,1)} %land_ref.1, f32[4,1,256]{2,1,0:T(1,128)} %bitcast.6, bf16[1024,256]{1,0:T(8,128)(2,1)} %vec_ref.1), custom_call_target="tpu_custom_call" | custom-call | tf_op jit(solution)/shard_map/prep/pallas_call | solution.py:48
  2.8 4.1 %collective-permute-start.3 = (bf16[272,768]{1,0:T(8,128)(2,1)}, bf16[272,768]{1,0:T(8,128)(2,1)S(1)}, u32[]{:S(2)}, u32[]{:S(2)}) collective-permute-start(bf16[272,768]{1,0:T(8,128)(2,1)} %get-tuple-element.52.refs_1_.refs_2_), channel_id=1, source_target_pairs={{0,4},{1,5},{2,6},{3,7},{4,0},{5,1},{6,2},{7,3},{8,12},{9,13},{10,... | collective-permute-start | bytes 1253384 | tf_op jit(solution)/shard_map/ppermute | solution.py:245
  6.9 1.5 %collective-permute-start.16 = (bf16[512,768]{1,0:T(8,128)(2,1)S(1)}, bf16[512,768]{1,0:T(8,128)(2,1)S(1)}, u32[]{:S(2)}, u32[]{:S(2)}) collective-permute-start(bf16[512,768]{1,0:T(8,128)(2,1)S(1)} %copy-done), channel_id=1, source_target_pairs={{0,8},{8,0},{16,24},{24,16},{1,9},{9,1},{17,25},{25,17},{2,10},{10... | collective-permute-start | bytes 2359304 | tf_op jit(solution)/shard_map/ppermute | solution.py:245
  8.4 1.5 %collective-permute-start.18 = (bf16[512,768]{1,0:T(8,128)(2,1)S(1)}, bf16[512,768]{1,0:T(8,128)(2,1)}, u32[]{:S(2)}, u32[]{:S(2)}) collective-permute-start(bf16[512,768]{1,0:T(8,128)(2,1)S(1)} %copy-done), channel_id=1, source_target_pairs={{0,16},{8,24},{16,0},{24,8},{1,17},{9,25},{17,1},{25,9},{2,18},{10... | collective-permute-start | bytes 2359304 | tf_op jit(solution)/shard_map/ppermute | solution.py:245
  9.9 1.6 %collective-permute-start.1 = (bf16[272,768]{1,0:T(8,128)(2,1)}, bf16[272,768]{1,0:T(8,128)(2,1)S(1)}, u32[]{:S(2)}, u32[]{:S(2)}) collective-permute-start(bf16[272,768]{1,0:T(8,128)(2,1)} %get-tuple-element.52.refs_1_.refs_2_), channel_id=1, source_target_pairs={{0,2},{1,3},{2,0},{3,1},{4,6},{5,7},{6,4},{7,5},{8,10},{9,11},{10,... | collective-permute-start | bytes 1253384 | tf_op jit(solution)/shard_map/ppermute | solution.py:245
  12.9 13.8 %collective-permute-done.3.refs_1_.refs_2_ = bf16[272,768]{1,0:T(8,128)(2,1)S(1)} collective-permute-done((bf16[272,768]{1,0:T(8,128)(2,1)}, bf16[272,768]{1,0:T(8,128)(2,1)S(1)}, u32[]{:S(2)}, u32[]{:S(2)}) %collective-permute-start.3) | collective-permute-done | bytes 417824 | tf_op jit(solution)/shard_map/ppermute | solution.py:245
  33.5 5.2 %collective-permute-done.5 = bf16[272,768]{1,0:T(8,128)(2,1)} collective-permute-done((bf16[272,768]{1,0:T(8,128)(2,1)S(1)}, bf16[272,768]{1,0:T(8,128)(2,1)}, u32[]{:S(2)}, u32[]{:S(2)}) %collective-permute-start.5) | collective-permute-done | bytes 417824 | tf_op jit(solution)/shard_map/ppermute | solution.py:263
  43.1 3.3 %block1_0.1 = (f32[512,512]{1,0:T(8,128)S(1)}, f32[512,512]{1,0:T(8,128)S(1)}, f32[1,512]{1,0:T(1,128)S(1)}, f32[1,512]{1,0:T(1,128)S(1)}, f32[1,512]{1,0:T(1,128)S(1)}) custom-call(bf16[512,768]{1,0:T(8,128)(2,1)S(1)} %copy-done.12, bf16[512,768]{1,0:T(8,128)(2,1)} %collective-permute-done.18.refs_1_, bf16[272,768]{1,0:T(8,128)(2,1)S(1)} %copy-done.2, ...), custom_call_target="tpu_custom_call" | custom-call | flops 805306368 | tf_op jit(solution)/shard_map/block1_0/pallas_call | solution.py:141
  46.5 2.5 %collective-permute-start.11 = (bf16[256,256]{1,0:T(8,128)(2,1)S(1)}, bf16[256,256]{1,0:T(8,128)(2,1)S(1)}, u32[]{:S(2)}, u32[]{:S(2)}) collective-permute-start(bf16[256,256]{1,0:T(8,128)(2,1)S(1)} %copy-done.1), channel_id=1, source_target_pairs={{0,4},{1,5},{2,6},{3,7},{4,0},{5,1},{6,2},{7,3},{8,12},{9,13},{10,... | collective-permute-start | bytes 393224 | tf_op jit(solution)/shard_map/ppermute | solution.py:245
  51.1 3.3 %block1_1.1 = (f32[512,512]{1,0:T(8,128)S(1)}, f32[512,512]{1,0:T(8,128)S(1)}, f32[1,512]{1,0:T(1,128)S(1)}, f32[1,512]{1,0:T(1,128)S(1)}, f32[1,512]{1,0:T(1,128)S(1)}) custom-call(bf16[512,768]{1,0:T(8,128)(2,1)S(1)} %copy-done.12, bf16[512,768]{1,0:T(8,128)(2,1)} %collective-permute-done.18.refs_1_, ...), custom_call_target="tpu_custom_call" | custom-call | flops 805306368 | tf_op jit(solution)/shard_map/block1_1/pallas_call | solution.py:141
  54.4 2.7 %collective-permute-start.9 = (bf16[256,256]{1,0:T(8,128)(2,1)S(1)}, bf16[256,256]{1,0:T(8,128)(2,1)S(1)}, u32[]{:S(2)}, u32[]{:S(2)}) collective-permute-start(bf16[256,256]{1,0:T(8,128)(2,1)S(1)} %copy-done.1), channel_id=1, source_target_pairs={{0,2},{1,3},{2,0},{3,1},{4,6},{5,7},{6,4},{7,5},{8,10},{9,11},{10,... | collective-permute-start | bytes 393224 | tf_op jit(solution)/shard_map/ppermute | solution.py:245
  59.0 3.3 %block1_2.1 = (f32[512,512]{1,0:T(8,128)S(1)}, f32[512,512]{1,0:T(8,128)S(1)}, f32[1,512]{1,0:T(1,128)S(1)}, f32[1,512]{1,0:T(1,128)S(1)}, f32[1,512]{1,0:T(1,128)S(1)}) custom-call(bf16[512,768]{1,0:T(8,128)(2,1)S(1)} %copy-done.12, bf16[512,768]{1,0:T(8,128)(2,1)} %collective-permute-done.18.refs_1_, ...), custom_call_target="tpu_custom_call" | custom-call | flops 805306368 | tf_op jit(solution)/shard_map/block1_2/pallas_call | solution.py:141
  69.7 3.3 %block1_3.1 = (f32[512,512]{1,0:T(8,128)S(1)}, f32[512,512]{1,0:T(8,128)S(1)}, f32[1,512]{1,0:T(1,128)S(1)}, f32[1,512]{1,0:T(1,128)S(1)}, f32[1,512]{1,0:T(1,128)S(1)}) custom-call(bf16[512,768]{1,0:T(8,128)(2,1)S(1)} %copy-done.12, bf16[512,768]{1,0:T(8,128)(2,1)} %collective-permute-done.18.refs_1_, ...), custom_call_target="tpu_custom_call" | custom-call | flops 805306368 | tf_op jit(solution)/shard_map/block1_3/pallas_call | solution.py:141
  75.1 2.6 %collective-permute-start.21 = (f32[4,512]{1,0:T(4,128)S(1)}, f32[4,512]{1,0:T(4,128)S(1)}, u32[]{:S(2)}, u32[]{:S(2)}) collective-permute-start(f32[4,512]{1,0:T(4,128)S(1)} %maximum_add_fusion.refs_12_), channel_id=1, source_target_pairs={{0,2},{1,3},{2,0},{3,1},{4,6},{5,7},{6,4},{7,5},{8,10},{9,11},{10,... | collective-permute-start | bytes 24584 | tf_op jit(solution)/shard_map/ppermute | solution.py:245
  78.0 2.2 %collective-permute-start.23 = (f32[4,512]{1,0:T(4,128)S(1)}, f32[4,512]{1,0:T(4,128)S(1)}, u32[]{:S(2)}, u32[]{:S(2)}) collective-permute-start(f32[4,512]{1,0:T(4,128)S(1)} %maximum_add_fusion.refs_12_), channel_id=1, source_target_pairs={{0,6},{1,7},{2,4},{3,5},{4,2},{5,3},{6,0},{7,1},{8,14},{9,15},{10,... | collective-permute-start | bytes 24584 | tf_op jit(solution)/shard_map/ppermute | solution.py:245
  80.2 2.1 %collective-permute-done.22.refs_14_ = f32[4,512]{1,0:T(4,128)S(1)} collective-permute-done((f32[4,512]{1,0:T(4,128)S(1)}, f32[4,512]{1,0:T(4,128)S(1)}, u32[]{:S(2)}, u32[]{:S(2)}) %collective-permute-start.22) | collective-permute-done | bytes 8224 | tf_op jit(solution)/shard_map/ppermute | solution.py:245
  84.9 1.5 %collective-permute-start.26 = (bf16[512,256]{1,0:T(8,128)(2,1)}, bf16[512,256]{1,0:T(8,128)(2,1)S(1)}, u32[]{:S(2)}, u32[]{:S(2)}) collective-permute-start(bf16[512,256]{1,0:T(8,128)(2,1)} %apply3.1), channel_id=1, source_target_pairs={{0,24},{8,16},{16,8},{24,0},{1,25},{9,17},{17,9},{25,1},{2,26},{10... | collective-permute-start | bytes 786440 | tf_op jit(solution)/shard_map/ppermute | solution.py:245
  89.7 1.5 %collective-permute-start.24 = (bf16[512,256]{1,0:T(8,128)(2,1)}, bf16[512,256]{1,0:T(8,128)(2,1)S(1)}, u32[]{:S(2)}, u32[]{:S(2)}) collective-permute-start(bf16[512,256]{1,0:T(8,128)(2,1)} %apply1.1), channel_id=1, source_target_pairs={{0,8},{8,0},{16,24},{24,16},{1,9},{9,1},{17,25},{25,17},{2,10},{10... | collective-permute-start | bytes 786440 | tf_op jit(solution)/shard_map/ppermute | solution.py:245
  91.2 1.5 %collective-permute-start.29 = (f32[1,512]{1,0:T(1,128)S(1)}, f32[1,512]{1,0:T(1,128)S(1)}, u32[]{:S(2)}, u32[]{:S(2)}) collective-permute-start(f32[1,512]{1,0:T(1,128)S(1)} %get-tuple-element.98), channel_id=1, source_target_pairs={{0,24},{8,16},{16,8},{24,0},{1,25},{9,17},{17,9},{25,1},{2,26},{10... | collective-permute-start | bytes 6152 | tf_op jit(solution)/shard_map/ppermute | solution.py:245
  94.2 4.7 %collective-permute-done.29.refs_7_ = f32[1,512]{1,0:T(1,128)S(1)} collective-permute-done((f32[1,512]{1,0:T(1,128)S(1)}, f32[1,512]{1,0:T(1,128)S(1)}, u32[]{:S(2)}, u32[]{:S(2)}) %collective-permute-start.29) | collective-permute-done | bytes 2080 | tf_op jit(solution)/shard_map/ppermute | solution.py:245
  107.7 3.7 %collective-permute-done.31 = bf16[128,256]{1,0:T(8,128)(2,1)S(1)} collective-permute-done((bf16[128,256]{1,0:T(8,128)(2,1)S(1)}, bf16[128,256]{1,0:T(8,128)(2,1)S(1)}, u32[]{:S(2)}, u32[]{:S(2)}) %collective-permute-start.31) | collective-permute-done | bytes 65568 | tf_op jit(solution)/shard_map/ppermute | solution.py:245
  112.1 3.7 %collective-permute-done.32 = bf16[128,256]{1,0:T(8,128)(2,1)S(1)} collective-permute-done((bf16[128,256]{1,0:T(8,128)(2,1)S(1)}, bf16[128,256]{1,0:T(8,128)(2,1)S(1)}, u32[]{:S(2)}, u32[]{:S(2)}) %collective-permute-start.32) | collective-permute-done | bytes 65568 | tf_op jit(solution)/shard_map/ppermute | solution.py:245
  115.9 4.2 %collective-permute-done.33 = bf16[128,256]{1,0:T(8,128)(2,1)S(1)} collective-permute-done((bf16[128,256]{1,0:T(8,128)(2,1)S(1)}, bf16[128,256]{1,0:T(8,128)(2,1)S(1)}, u32[]{:S(2)}, u32[]{:S(2)}) %collective-permute-start.33) | collective-permute-done | bytes 65568 | tf_op jit(solution)/shard_map/ppermute | solution.py:245
  120.8 4.8 %collective-permute-done.34 = bf16[128,256]{1,0:T(8,128)(2,1)S(1)} collective-permute-done((bf16[128,256]{1,0:T(8,128)(2,1)S(1)}, bf16[128,256]{1,0:T(8,128)(2,1)S(1)}, u32[]{:S(2)}, u32[]{:S(2)}) %collective-permute-start.34) | collective-permute-done | bytes 65568 | tf_op jit(solution)/shard_map/ppermute | solution.py:245
  (109 shorter events, 46.3 us)
Async XLA Ops:
  2.8 23.8 %collective-permute-start.3 = (bf16[272,768]{1,0:T(8,128)(2,1)}, bf16[272,768]{1,0:T(8,128)(2,1)S(1)}, u32[]{:S(2)}, u32[]{:S(2)}) collective-permute-start(bf16[272,768]{1,0:T(8,128)(2,1)} %get-tuple-element.52.refs_1_.refs_2_), channel_id=1, source_target_pairs={{0,4},{1,5},{2,6},{3,7},{4,0},{5,1},{6,2},{7,3},{8,12},{9,13},{10,... | collective-permute-start | bytes 1253384 | tf_op jit(solution)/shard_map/ppermute | solution.py:245
  6.9 21.6 %collective-permute-start.16 = (bf16[512,768]{1,0:T(8,128)(2,1)S(1)}, bf16[512,768]{1,0:T(8,128)(2,1)S(1)}, u32[]{:S(2)}, u32[]{:S(2)}) collective-permute-start(bf16[512,768]{1,0:T(8,128)(2,1)S(1)} %copy-done), channel_id=1, source_target_pairs={{0,8},{8,0},{16,24},{24,16},{1,9},{9,1},{17,25},{25,17},{2,10},{10... | collective-permute-start | bytes 2359304 | tf_op jit(solution)/shard_map/ppermute | solution.py:245
  8.4 22.6 %collective-permute-start.18 = (bf16[512,768]{1,0:T(8,128)(2,1)S(1)}, bf16[512,768]{1,0:T(8,128)(2,1)}, u32[]{:S(2)}, u32[]{:S(2)}) collective-permute-start(bf16[512,768]{1,0:T(8,128)(2,1)S(1)} %copy-done), channel_id=1, source_target_pairs={{0,16},{8,24},{16,0},{24,8},{1,17},{9,25},{17,1},{25,9},{2,18},{10... | collective-permute-start | bytes 2359304 | tf_op jit(solution)/shard_map/ppermute | solution.py:245
  9.9 18.6 %collective-permute-start.1 = (bf16[272,768]{1,0:T(8,128)(2,1)}, bf16[272,768]{1,0:T(8,128)(2,1)S(1)}, u32[]{:S(2)}, u32[]{:S(2)}) collective-permute-start(bf16[272,768]{1,0:T(8,128)(2,1)} %get-tuple-element.52.refs_1_.refs_2_), channel_id=1, source_target_pairs={{0,2},{1,3},{2,0},{3,1},{4,6},{5,7},{6,4},{7,5},{8,10},{9,11},{10,... | collective-permute-start | bytes 1253384 | tf_op jit(solution)/shard_map/ppermute | solution.py:245
  11.5 20.6 %collective-permute-start.6 = (bf16[272,768]{1,0:T(8,128)(2,1)}, bf16[272,768]{1,0:T(8,128)(2,1)}, u32[]{:S(2)}, u32[]{:S(2)}) collective-permute-start(bf16[272,768]{1,0:T(8,128)(2,1)} %get-tuple-element.52.refs_1_.refs_2_), channel_id=1, source_target_pairs={{2,4},{3,5},{4,2},{5,3},{10,12},{11,13},{12,10},{13,11},{18,20},{1... | collective-permute-start | bytes 1253384 | tf_op jit(solution)/shard_map/ppermute | solution.py:262
  26.7 11.9 %collective-permute-start.5 = (bf16[272,768]{1,0:T(8,128)(2,1)S(1)}, bf16[272,768]{1,0:T(8,128)(2,1)}, u32[]{:S(2)}, u32[]{:S(2)}) collective-permute-start(bf16[272,768]{1,0:T(8,128)(2,1)S(1)} %collective-permute-done.3.refs_1_.refs_2_), channel_id=1, source_target_pairs={{4,6},{5,7},{2,0},{3,1},{12,14},{13,15},{10,8},{11,9},{20,22},{21,... | collective-permute-start | bytes 1253384 | tf_op jit(solution)/shard_map/ppermute | solution.py:263
  28.5 12.4 %collective-permute-start = (bf16[272,768]{1,0:T(8,128)(2,1)}, bf16[272,768]{1,0:T(8,128)(2,1)S(1)}, u32[]{:S(2)}, u32[]{:S(2)}) collective-permute-start(bf16[272,768]{1,0:T(8,128)(2,1)} %get-tuple-element.52.refs_1_.refs_2_), channel_id=1, source_target_pairs={{0,1},{1,0},{2,3},{3,2},{4,5},{5,4},{6,7},{7,6},{8,9},{9,8},{10,11... | collective-permute-start | bytes 1253384 | tf_op jit(solution)/shard_map/ppermute | solution.py:245
  29.4 17.0 %collective-permute-start.2 = (bf16[272,768]{1,0:T(8,128)(2,1)S(1)}, bf16[272,768]{1,0:T(8,128)(2,1)S(1)}, u32[]{:S(2)}, u32[]{:S(2)}) collective-permute-start(bf16[272,768]{1,0:T(8,128)(2,1)S(1)} %collective-permute-done.1.refs_1_.refs_2_), channel_id=1, source_target_pairs={{0,1},{1,0},{2,3},{3,2},{4,5},{5,4},{6,7},{7,6},{8,9},{9,8},{10,11... | collective-permute-start | bytes 1253384 | tf_op jit(solution)/shard_map/ppermute | solution.py:245
  31.0 23.4 %collective-permute-start.4 = (bf16[272,768]{1,0:T(8,128)(2,1)S(1)}, bf16[272,768]{1,0:T(8,128)(2,1)S(1)}, u32[]{:S(2)}, u32[]{:S(2)}) collective-permute-start(bf16[272,768]{1,0:T(8,128)(2,1)S(1)} %collective-permute-done.3.refs_1_.refs_2_), channel_id=1, source_target_pairs={{0,1},{1,0},{2,3},{3,2},{4,5},{5,4},{6,7},{7,6},{8,9},{9,8},{10,11... | collective-permute-start | bytes 1253384 | tf_op jit(solution)/shard_map/ppermute | solution.py:245
  32.1 30.9 %collective-permute-start.17 = (bf16[256,768]{1,0:T(8,128)(2,1)S(1)}, bf16[256,768]{1,0:T(8,128)(2,1)S(1)}, u32[]{:S(2)}, u32[]{:S(2)}) collective-permute-start(bf16[256,768]{1,0:T(8,128)(2,1)S(1)} %slice.16), channel_id=1, source_target_pairs={{0,16},{8,24},{16,0},{24,8},{1,17},{9,25},{17,1},{25,9},{2,18},{10... | collective-permute-start | bytes 1179656 | tf_op jit(solution)/shard_map/ppermute | solution.py:245
  38.6 24.5 %collective-permute-start.19 = (bf16[256,768]{1,0:T(8,128)(2,1)S(1)}, bf16[256,768]{1,0:T(8,128)(2,1)S(1)}, u32[]{:S(2)}, u32[]{:S(2)}) collective-permute-start(bf16[256,768]{1,0:T(8,128)(2,1)S(1)} %slice.17), channel_id=1, source_target_pairs={{0,8},{8,0},{16,24},{24,16},{1,9},{9,1},{17,25},{25,17},{2,10},{10... | collective-permute-start | bytes 1179656 | tf_op jit(solution)/shard_map/ppermute | solution.py:245
  40.9 26.6 %collective-permute-start.7 = (bf16[272,768]{1,0:T(8,128)(2,1)S(1)}, bf16[272,768]{1,0:T(8,128)(2,1)S(1)}, u32[]{:S(2)}, u32[]{:S(2)}) collective-permute-start(bf16[272,768]{1,0:T(8,128)(2,1)S(1)} %broadcast_select_fusion.refs_1_.refs_2_), channel_id=1, source_target_pairs={{0,1},{1,0},{2,3},{3,2},{4,5},{5,4},{6,7},{7,6},{8,9},{9,8},{10,11... | collective-permute-start | bytes 1253384 | tf_op jit(solution)/shard_map/ppermute | solution.py:245
  46.5 15.8 %collective-permute-start.11 = (bf16[256,256]{1,0:T(8,128)(2,1)S(1)}, bf16[256,256]{1,0:T(8,128)(2,1)S(1)}, u32[]{:S(2)}, u32[]{:S(2)}) collective-permute-start(bf16[256,256]{1,0:T(8,128)(2,1)S(1)} %copy-done.1), channel_id=1, source_target_pairs={{0,4},{1,5},{2,6},{3,7},{4,0},{5,1},{6,2},{7,3},{8,12},{9,13},{10,... | collective-permute-start | bytes 393224 | tf_op jit(solution)/shard_map/ppermute | solution.py:245
  54.4 12.6 %collective-permute-start.9 = (bf16[256,256]{1,0:T(8,128)(2,1)S(1)}, bf16[256,256]{1,0:T(8,128)(2,1)S(1)}, u32[]{:S(2)}, u32[]{:S(2)}) collective-permute-start(bf16[256,256]{1,0:T(8,128)(2,1)S(1)} %copy-done.1), channel_id=1, source_target_pairs={{0,2},{1,3},{2,0},{3,1},{4,6},{5,7},{6,4},{7,5},{8,10},{9,11},{10,... | collective-permute-start | bytes 393224 | tf_op jit(solution)/shard_map/ppermute | solution.py:245
  62.3 11.5 %collective-permute-start.14 = (bf16[256,256]{1,0:T(8,128)(2,1)S(1)}, bf16[256,256]{1,0:T(8,128)(2,1)S(1)}, u32[]{:S(2)}, u32[]{:S(2)}) collective-permute-start(bf16[256,256]{1,0:T(8,128)(2,1)S(1)} %copy-done.1), channel_id=1, source_target_pairs={{2,4},{3,5},{4,2},{5,3},{10,12},{11,13},{12,10},{13,11},{18,20},{1... | collective-permute-start | bytes 393224 | tf_op jit(solution)/shard_map/ppermute | solution.py:262
  63.0 14.7 %collective-permute-start.8 = (bf16[256,256]{1,0:T(8,128)(2,1)S(1)}, bf16[256,256]{1,0:T(8,128)(2,1)S(1)}, u32[]{:S(2)}, u32[]{:S(2)}) collective-permute-start(bf16[256,256]{1,0:T(8,128)(2,1)S(1)} %copy-done.1), channel_id=1, source_target_pairs={{0,1},{1,0},{2,3},{3,2},{4,5},{5,4},{6,7},{7,6},{8,9},{9,8},{10,11... | collective-permute-start | bytes 393224 | tf_op jit(solution)/shard_map/ppermute | solution.py:245
  63.1 11.2 %collective-permute-start.13 = (bf16[256,256]{1,0:T(8,128)(2,1)S(1)}, bf16[256,256]{1,0:T(8,128)(2,1)S(1)}, u32[]{:S(2)}, u32[]{:S(2)}) collective-permute-start(bf16[256,256]{1,0:T(8,128)(2,1)S(1)} %collective-permute-done.11.refs_8_), channel_id=1, source_target_pairs={{4,6},{5,7},{2,0},{3,1},{12,14},{13,15},{10,8},{11,9},{20,22},{21,... | collective-permute-start | bytes 393224 | tf_op jit(solution)/shard_map/ppermute | solution.py:263
  67.0 13.2 %collective-permute-start.12 = (bf16[256,256]{1,0:T(8,128)(2,1)S(1)}, bf16[256,256]{1,0:T(8,128)(2,1)S(1)}, u32[]{:S(2)}, u32[]{:S(2)}) collective-permute-start(bf16[256,256]{1,0:T(8,128)(2,1)S(1)} %collective-permute-done.11.refs_8_), channel_id=1, source_target_pairs={{0,1},{1,0},{2,3},{3,2},{4,5},{5,4},{6,7},{7,6},{8,9},{9,8},{10,11... | collective-permute-start | bytes 393224 | tf_op jit(solution)/shard_map/ppermute | solution.py:245
  67.5 10.5 %collective-permute-start.10 = (bf16[256,256]{1,0:T(8,128)(2,1)S(1)}, bf16[256,256]{1,0:T(8,128)(2,1)S(1)}, u32[]{:S(2)}, u32[]{:S(2)}) collective-permute-start(bf16[256,256]{1,0:T(8,128)(2,1)S(1)} %collective-permute-done.9.refs_6_), channel_id=1, source_target_pairs={{0,1},{1,0},{2,3},{3,2},{4,5},{5,4},{6,7},{7,6},{8,9},{9,8},{10,11... | collective-permute-start | bytes 393224 | tf_op jit(solution)/shard_map/ppermute | solution.py:245
  84.9 19.9 %collective-permute-start.26 = (bf16[512,256]{1,0:T(8,128)(2,1)}, bf16[512,256]{1,0:T(8,128)(2,1)S(1)}, u32[]{:S(2)}, u32[]{:S(2)}) collective-permute-start(bf16[512,256]{1,0:T(8,128)(2,1)} %apply3.1), channel_id=1, source_target_pairs={{0,24},{8,16},{16,8},{24,0},{1,25},{9,17},{17,9},{25,1},{2,26},{10... | collective-permute-start | bytes 786440 | tf_op jit(solution)/shard_map/ppermute | solution.py:245
  87.8 17.0 %collective-permute-start.25 = (bf16[512,256]{1,0:T(8,128)(2,1)}, bf16[512,256]{1,0:T(8,128)(2,1)S(1)}, u32[]{:S(2)}, u32[]{:S(2)}) collective-permute-start(bf16[512,256]{1,0:T(8,128)(2,1)} %apply2.1), channel_id=1, source_target_pairs={{0,16},{8,24},{16,0},{24,8},{1,17},{9,25},{17,1},{25,9},{2,18},{10... | collective-permute-start | bytes 786440 | tf_op jit(solution)/shard_map/ppermute | solution.py:245
  89.7 15.0 %collective-permute-start.24 = (bf16[512,256]{1,0:T(8,128)(2,1)}, bf16[512,256]{1,0:T(8,128)(2,1)S(1)}, u32[]{:S(2)}, u32[]{:S(2)}) collective-permute-start(bf16[512,256]{1,0:T(8,128)(2,1)} %apply1.1), channel_id=1, source_target_pairs={{0,8},{8,0},{16,24},{24,16},{1,9},{9,1},{17,25},{25,17},{2,10},{10... | collective-permute-start | bytes 786440 | tf_op jit(solution)/shard_map/ppermute | solution.py:245
  91.2 7.6 %collective-permute-start.29 = (f32[1,512]{1,0:T(1,128)S(1)}, f32[1,512]{1,0:T(1,128)S(1)}, u32[]{:S(2)}, u32[]{:S(2)}) collective-permute-start(f32[1,512]{1,0:T(1,128)S(1)} %get-tuple-element.98), channel_id=1, source_target_pairs={{0,24},{8,16},{16,8},{24,0},{1,25},{9,17},{17,9},{25,1},{2,26},{10... | collective-permute-start | bytes 6152 | tf_op jit(solution)/shard_map/ppermute | solution.py:245
  92.7 12.0 %collective-permute-start.27 = (f32[1,512]{1,0:T(1,128)S(1)}, f32[1,512]{1,0:T(1,128)S(1)}, u32[]{:S(2)}, u32[]{:S(2)}) collective-permute-start(f32[1,512]{1,0:T(1,128)S(1)} %get-tuple-element.96), channel_id=1, source_target_pairs={{0,8},{8,0},{16,24},{24,16},{1,9},{9,1},{17,25},{25,17},{2,10},{10... | collective-permute-start | bytes 6152 | tf_op jit(solution)/shard_map/ppermute | solution.py:245
  (26 other events, 129.4 us)

commit v2 on v1

v2 whole, which is shorter than its diff:
```python
import functools
import math

import jax
import jax.numpy as jnp
from jax import lax
from jax.experimental import pallas as pl
from jax.experimental.pallas import tpu as pltpu
from jax.sharding import PartitionSpec as P

F32 = jnp.float32
B16 = jnp.bfloat16
EXTRA = 16
VMEM = pl.BlockSpec(memory_space=pltpu.VMEM)
SMEM = pl.BlockSpec(memory_space=pltpu.SMEM)
LIMIT = 8 << 20
TRANS = (((1,), (1,)), ((), ()))


def split3(x):
    hi = x.astype(B16)
    rest = x - hi.astype(F32)
    mid = rest.astype(B16)
    return hi, mid, (rest - mid.astype(F32)).astype(B16)


def prep_body(pos_ref, land_ref, scale_ref, vec_ref, msg_ref, vmsg_ref):
    stripe, depth = land_ref.shape
    msg_ref[stripe:, :] = jnp.zeros((EXTRA, depth), B16)
    land = land_ref[...]
    msg_ref[:stripe, :] = land
    vmsg_ref[...] = vec_ref[...]
    vals = land.astype(F32)
    squares = vals * vals
    high = squares.astype(B16)
    low = (squares - high.astype(F32)).astype(B16)
    ones = jnp.ones((8, depth), B16)
    norm = lax.dot_general(ones, high, TRANS, preferred_element_type=F32)
    norm = norm + lax.dot_general(ones, low, TRANS, preferred_element_type=F32)
    rows = split3(scale_ref[0]) + split3(norm[:1])
    block = jnp.concatenate([r.astype(F32) for r in rows] + [jnp.zeros((EXTRA - 6, stripe), F32)], axis=0)
    msg_ref[stripe:, :stripe] = block.astype(B16)


def in_hbm(x):
    return pltpu.with_memory_space_constraint(x, pltpu.HBM)


def prep(pos, landmarks, scales, eigvecs, parts):
    count, depth = landmarks.shape
    stripe = count // parts
    width = eigvecs.shape[1]
    return pl.pallas_call(
        prep_body,
        grid_spec=pltpu.PrefetchScalarGridSpec(
            num_scalar_prefetch=1,
            grid=(1,),
            in_specs=[
                pl.BlockSpec((stripe, depth), lambda i, p: (p[0], 0)),
                pl.BlockSpec((1, 1, stripe), lambda i, p: (p[0], 0, 0)),
                pl.BlockSpec((stripe, width), lambda i, p: (p[0], 0)),
            ],
            out_specs=[
                pl.BlockSpec((stripe + EXTRA, depth), lambda i, p: (0, 0)),
                pl.BlockSpec((stripe, width), lambda i, p: (0, 0)),
            ],
        ),
        out_shape=[
            jax.ShapeDtypeStruct((stripe + EXTRA, depth), B16),
            jax.ShapeDtypeStruct((stripe, width), B16),
        ],
        compiler_params=pltpu.CompilerParams(vmem_limit_bytes=LIMIT),
        name="prep",
    )(pos, in_hbm(landmarks), scales.reshape(parts, 1, stripe), in_hbm(eigvecs))


def block_body(*refs, groups):
    nrow = sum(groups)
    rows = refs[:nrow]
    msgs = refs[nrow : nrow + 2]
    col_in = refs[nrow + 2]
    row_in = refs[nrow + 3 : nrow + 3 + len(groups)]
    outs = refs[nrow + 3 + len(groups) :]
    kern = outs[: len(groups)]
    col_out = outs[len(groups)]
    row_out = outs[len(groups) + 1 :]
    stripe = msgs[0].shape[0] - EXTRA
    log2e = math.log2(math.e)

    def triple(ref, at):
        part = ref[stripe:, :stripe].astype(F32)
        return part[at : at + 1] + part[at + 1 : at + 2] + part[at + 2 : at + 3]

    neg = [triple(m, 0) * (-log2e) for m in msgs]
    norm = [triple(m, 3) for m in msgs]
    cols = [jnp.zeros((8, stripe), F32) for _ in msgs]
    at = 0
    for g, pieces in enumerate(groups):
        base = 0
        for _ in range(pieces):
            src = rows[at]
            at += 1

            size = src.shape[0]
            block = src[...]
            vals = block.astype(F32)
            sq = jnp.sum(vals * vals, axis=1, keepdims=True)
            lanes = jnp.zeros((size, 128), F32)
            for e, m in enumerate(msgs):
                cross = lax.dot_general(block, m[:stripe, :], TRANS, preferred_element_type=F32)
                dist = (sq + norm[e]) - 2.0 * cross
                value = jnp.exp2(dist * neg[e])
                kern[g][base : base + size, e * stripe : (e + 1) * stripe] = value
                cols[e] = cols[e] + jnp.sum(value.reshape(size // 8, 8, stripe), axis=0)
                for q in range(stripe // 128):
                    lanes = lanes + value[:, q * 128 : (q + 1) * 128]
            for q in range(size // 128):
                row = jnp.sum(lanes[q * 128 : (q + 1) * 128].T, axis=0, keepdims=True)
                spot = slice(base + q * 128, base + (q + 1) * 128)
                row_out[g][:, spot] = row_in[g][:, spot] + row
            base += size
    total = jnp.concatenate([jnp.sum(c, axis=0, keepdims=True) for c in cols], axis=1)
    col_out[...] = col_in[...] + total


def block_call(row_groups, msgs, col_in, row_in):
    groups = tuple(len(g) for g in row_groups)
    flat = [r for g in row_groups for r in g]
    depth = flat[0].shape[1]
    stripe = msgs[0].shape[0] - EXTRA
    sizes = [sum(r.shape[0] for r in g) for g in row_groups]
    out_shape = (
        [jax.ShapeDtypeStruct((n, 2 * stripe), F32) for n in sizes]
        + [jax.ShapeDtypeStruct((1, 2 * stripe), F32)]
        + [jax.ShapeDtypeStruct((1, n), F32) for n in sizes]
    )
    flops = 2 * sum(sizes) * 2 * stripe * depth
    outs = pl.pallas_call(
        functools.partial(block_body, groups=groups),
        out_shape=out_shape,
        in_specs=[VMEM] * (len(flat) + 2 + 1 + len(groups)),
        out_specs=[VMEM] * len(out_shape),
        cost_estimate=pl.CostEstimate(flops=flops, bytes_accessed=0, transcendentals=sum(sizes) * 2 * stripe),
        compiler_params=pltpu.CompilerParams(vmem_limit_bytes=LIMIT),
    )(*flat, *msgs, col_in, *row_in)
    n = len(groups)
    return outs[:n], outs[n], outs[n + 1 :]


def apply_body(*refs, slots, peers, tail):
    kern = refs[:slots]
    vecs = refs[slots : 3 * slots]
    degs = refs[3 * slots : 3 * slots + 1 + peers]
    out = refs[-1]
    stripe, width = vecs[0].shape
    rows = kern[0].shape[0]
    acc = None
    for k in range(slots):
        total = degs[0][k : k + 1, :]
        for j in range(1, peers + 1):
            total = total + degs[j][k ^ j : (k ^ j) + 1, :]
        weight = lax.rsqrt(total)
        for e in range(2):
            span = slice(e * stripe, (e + 1) * stripe)
            scaled = (kern[k][:, span] * weight[:, span]).astype(B16)
            term = jnp.dot(scaled, vecs[2 * k + e][...], preferred_element_type=F32)
            acc = term if acc is None else acc + term
    out[:rows, :] = acc.astype(out.dtype)
    if tail:
        sums = refs[-2]
        parts = []
        for at in range(0, rows, width):
            parts += [p.astype(F32) for p in split3(sums[:, at : at + width])]
        parts.append(jnp.zeros((EXTRA - len(parts), width), F32))
        out[rows:, :] = jnp.concatenate(parts, axis=0).astype(B16)


def apply_call(kern, vecs, degs, row_sum):
    rows = kern[0].shape[0]
    width = vecs[0].shape[1]
    tail = row_sum is not None
    operands = [*kern, *vecs, *degs] + ([row_sum] if tail else [])
    flops = 2 * rows * width * sum(v.shape[0] for v in vecs)
    return pl.pallas_call(
        functools.partial(apply_body, slots=len(kern), peers=len(degs) - 1, tail=tail),
        out_shape=jax.ShapeDtypeStruct((rows + EXTRA * tail, width), B16 if tail else F32),
        in_specs=[VMEM] * len(operands),
        out_specs=VMEM,
        cost_estimate=pl.CostEstimate(flops=flops, bytes_accessed=0, transcendentals=0),
        compiler_params=pltpu.CompilerParams(vmem_limit_bytes=LIMIT),
    )(*operands)


def finish_body(core_ref, *refs, parts, factor):
    sums = refs[:parts]
    deg_ref, eig_ref, coords_ref, keep_ref, send_ref = refs[parts:]
    rows, width = coords_ref.shape
    half = width // 2
    deg = deg_ref[...]
    for s in sums[1:]:
        tail = s[rows:, :].astype(F32)
        pieces = [tail[3 * i : 3 * i + 1] + tail[3 * i + 1 : 3 * i + 2] + tail[3 * i + 2 : 3 * i + 3] for i in range(rows // width)]
        deg = deg + jnp.concatenate(pieces, axis=1)
    gain = factor / jnp.sqrt(deg)
    inv = 1.0 / eig_ref[...]
    highs, lows = [], []
    for q in range(rows // 128):
        span = slice(q * 128, (q + 1) * 128)
        column = jnp.broadcast_to(gain[:, span], (128, 128)).T
        total = sums[0][span, :].astype(F32)
        for s in sums[1:]:
            total = total + s[span, :].astype(F32)
        value = jnp.concatenate(
            [total[:, k * 128 : (k + 1) * 128] * column for k in range(width // 128)], axis=1
        ) * inv
        coords_ref[span, :] = value
        high = value.astype(B16)
        highs.append(high)
        lows.append((value - high.astype(F32)).astype(B16))
    high = jnp.concatenate(highs, axis=0)
    low = jnp.concatenate(lows, axis=0)
    dims = (((0,), (0,)), ((), ()))
    outer = lax.dot_general(high, high, dims, preferred_element_type=F32)
    outer = outer + lax.dot_general(high, low, dims, preferred_element_type=F32)
    outer = outer + lax.dot_general(low, high, dims, preferred_element_type=F32)
    first = core_ref[1] == 0
    top, bottom = outer[:half], outer[half:]
    keep_ref[...] = jnp.where(first, top, bottom)
    send_ref[...] = jnp.where(first, bottom, top).astype(B16)


def finish_call(core, sums, deg, eigvals, factor):
    rows, width = sums[0].shape
    return pl.pallas_call(
        functools.partial(finish_body, parts=len(sums), factor=factor),
        out_shape=[
            jax.ShapeDtypeStruct((rows, width), F32),
            jax.ShapeDtypeStruct((width // 2, width), F32),
            jax.ShapeDtypeStruct((width // 2, width), B16),
        ],
        in_specs=[SMEM] + [VMEM] * (len(sums) + 2),
        out_specs=[VMEM] * 3,
        compiler_params=pltpu.CompilerParams(vmem_limit_bytes=LIMIT),
        name="finish",
    )(core, *sums, deg, eigvals.reshape(1, width))


def join_body(core_ref, own_ref, other_ref, out_ref, *, scale):
    half = own_ref.shape[0]
    first = core_ref[1] == 0
    own, other = own_ref[...] * scale, other_ref[...] * scale
    out_ref[:half] = jnp.where(first, own, other)
    out_ref[half:] = jnp.where(first, other, own)


def join_call(core, own, other, scale):
    half, width = own.shape
    return pl.pallas_call(
        functools.partial(join_body, scale=scale),
        out_shape=jax.ShapeDtypeStruct((2 * half, width), F32),
        in_specs=[SMEM, VMEM, VMEM],
        out_specs=VMEM,
        compiler_params=pltpu.CompilerParams(vmem_limit_bytes=LIMIT),
        name="join",
    )(core, own, other)


def exchange(x, axis, offset):
    size = lax.axis_size(axis)
    return lax.ppermute(x, axis, [(i, i ^ offset) for i in range(size)])


def after(x, *others):
    return lax.optimization_barrier((x, *others))[0]


def per_device(items, landmarks, scales, eigvecs, eigvals):
    dp = lax.axis_size("dp")
    land = lax.axis_size("land")
    chips = land // 2
    own = items.shape[0]
    rows_all = own * dp * land
    landmark_count = landmarks.shape[0] * land
    pos = jnp.stack([lax.axis_index("dp"), lax.axis_index("land") & 1]).astype(jnp.int32)
    small = dp == 4 and chips == 4

    kern = [[None] * chips for _ in range(dp)]
    row = [jnp.zeros((1, own), F32) for _ in range(dp)]
    token = [None]

    def block(group, k, mine, mates, col):
        if token[0] is not None:
            col[k] = after(col[k], token[0])
        out, col[k], rows_out = block_call(
            [row_sets[d] for d in group], (mine[k], mates[k]), col[k], [row[d] for d in group]
        )
        for i, d in enumerate(group):
            kern[d][k] = out[i]
            row[d] = rows_out[i]
        token[0] = col[k]

    def line_gather(x, ready=None):
        if chips != 4:
            return [x] + [exchange(x, "land", 2 * k) for k in range(1, chips)]
        two = exchange(x, "land", 4)
        one = exchange(x, "land", 2)
        inner = lax.ppermute(x, "land", [(2, 4), (3, 5), (4, 2), (5, 3)])
        relay = two if ready is None else after(two, *ready())
        outer = lax.ppermute(relay, "land", [(4, 6), (5, 7), (2, 0), (3, 1)])
        return [x, one, two, inner + outer]

    mates = [None] * chips
    if small:
        half = own // 2
        upper, lower = items[:half], items[half:]
        row_sets = [[items], [exchange(upper, "dp", 1)], [exchange(lower, "dp", 2)]]
        msg, vmsg = prep(pos, landmarks, scales, eigvecs, dp)
        stripe = vmsg.shape[0]
        col = [jnp.zeros((1, 2 * stripe), F32) for _ in range(chips)]
        mates[0] = exchange(msg, "land", 1)
        mine = [msg]
        row_sets[1].append(exchange(lower, "dp", 1))
        row_sets[2].insert(0, exchange(upper, "dp", 2))
        row_sets.append([exchange(row_sets[1][0], "dp", 2), exchange(row_sets[2][1], "dp", 1)])
        block([0], 0, mine, mates, col)
        block([1, 2], 0, mine, mates, col)
        seen = token[0]
        mine = line_gather(msg, lambda: (seen,))
        for k in (2, 1):
            mates[k] = exchange(mine[k], "land", 1)
            block([0], k, mine, mates, col)
            block([1, 2], k, mine, mates, col)
        vmine = line_gather(after(vmsg, token[0]))
        for k in (0, 2, 1):
            block([3], k, mine, mates, col)
        mates[3] = exchange(mine[3], "land", 1)
        for group in ([0], [1, 2], [3]):
            block(group, 3, mine, mates, col)
    else:
        row_sets = [[items]] + [[exchange(items, "dp", d)] for d in range(1, dp)]
        msg, vmsg = prep(pos, landmarks, scales, eigvecs, dp)
        stripe = vmsg.shape[0]
        col = [jnp.zeros((1, 2 * stripe), F32) for _ in range(chips)]
        mine = line_gather(msg)
        mates = [exchange(m, "land", 1) for m in mine]
        vmine = line_gather(vmsg)
        for d in range(dp):
            for k in range(chips):
                block([d], k, mine, mates, col)
    vmates = [exchange(m, "land", 1) for m in vmine]

    deg = jnp.concatenate(col, axis=0)
    mate = exchange(deg, "land", 1)
    deg = deg + jnp.concatenate([mate[:, stripe:], mate[:, :stripe]], axis=1)
    degs = [deg] + [exchange(deg, "land", 2 * k) for k in range(chips - 1, 0, -1)][::-1]
    vecs = [v for pair in zip(vmine, vmates) for v in pair]

    sums = [None] * dp
    last = None
    for d in list(range(dp - 1, 0, -1)) + [0]:
        if last is not None:
            degs = [after(degs[0], last)] + degs[1:]
        part = apply_call(kern[d], vecs, degs, row[d] if d else None)
        last = part
        sums[d] = exchange(part, "dp", d) if d else part

    factor = math.sqrt(float(rows_all) * float(landmark_count))
    coords, keep, send = finish_call(pos, sums, row[0], eigvals, factor)
    total = keep + exchange(send, "land", 1).astype(F32)
    for axis, size in (("dp", dp), ("land", land)):
        step = 1 if axis == "dp" else 2
        while step < size:
            total = lax.reduce_precision(total, 8, 7)
            total = total + exchange(total.astype(B16), axis, step).astype(F32)
            step *= 2
    other = exchange(total, "land", 1)
    gram = join_call(pos, total, other, 1.0 / rows_all)
    return (coords, gram)


def solution(mesh):
    return jax.shard_map(
        per_device,
        mesh=mesh,
        in_specs=(P(("dp", "land"), None), P("land", None), P("land"), P("land", None), P()),
        out_specs=(P(("dp", "land"), None), P()),
        check_vma=False,
    )
```

time: 128 us -> 120 us (0.938)
  waiting for transfers between devices: 47.2 us -> 60.5 us
  local copies, waits for them, and re-layouts: 10.6 us -> 1.26 us
  Pallas kernels: 28.8 us -> 19.8 us
  starting transfers between devices: 38.3 us -> 36.5 us
  other arithmetic: 1.99 us -> 0.38 us
    ppermute x32 -> x31, waiting for transfers between devices: 42 us -> 52.8 us  [exchange(): return lax.ppermute(x, axis, [(i, i ^ offset) for i in range(size)])]
    unnamed x28 -> x6, local copies, waits for them, and re-layouts: 8.56 us -> 0.01 us
    pallas_call x12 -> x13, Pallas kernels: 20.6 us -> 13.4 us  [the longest x12 12.1 us: block_call(): pl.pallas_call(functools.partial(block_body, groups=groups), out_shape=ou...]
    ppermute x4, waiting for transfers between devices: 5.16 us -> 7.77 us  [the longest x2 7.77 us: line_gather(): outer = lax.ppermute(relay, 'land', [(4, 6), (5, 7), (2, 0), (3, 1)])]
    pallas_call x4, Pallas kernels: 5 us -> 2.94 us  [apply_call(): pl.pallas_call(functools.partial(apply_body, slots=len(kern), peers=len(d...]
    ppermute x32 -> x31, starting transfers between devices: 33.4 us -> 32.4 us  [exchange(): return lax.ppermute(x, axis, [(i, i ^ offset) for i in range(size)])]
  transfers between devices with their start and end apart: 36 -> 35, of which waited for: 13 -> 17; matrix products, arithmetic and copies ran while one was open for 2% -> 0% of each run, Pallas kernels for 19% -> 12%
where the time goes in v2:
time: 120 us; the launch traced here: 119 us
  waiting for transfers between devices  60.5 us (50%)
  starting transfers between devices  36.5 us (30%)
  Pallas kernels  19.8 us (16%)
  local copies, waits for them, and re-layouts  1.26 us (1%)
    ppermute x31, waiting for transfers between devices, exchange(): return lax.ppermute(x, axis, [(i, i ^ offset) for i in range(size)])  52.8 us
    ppermute x31, starting transfers between devices, exchange(): return lax.ppermute(x, axis, [(i, i ^ offset) for i in range(size)])  32.4 us
    pallas_call x12, Pallas kernels, block_call(): pl.pallas_call(functools.partial(block_body, groups=groups), out_shape=ou...  12.1 us
    ppermute x2, waiting for transfers between devices, line_gather(): outer = lax.ppermute(relay, 'land', [(4, 6), (5, 7), (2, 0), (3, 1)])  7.77 us
    pallas_call x4, Pallas kernels, apply_call(): pl.pallas_call(functools.partial(apply_body, slots=len(kern), peers=len(d...  2.94 us
    ppermute x2, starting transfers between devices, line_gather(): outer = lax.ppermute(relay, 'land', [(4, 6), (5, 7), (2, 0), (3, 1)])  2.74 us
  transfers between devices with their start and end apart: 35, of which 17 were waited for; matrix products, arithmetic and copies ran while one was open for 0% of the time, Pallas kernels for 12%

profile of v2, /device:TPU:0, one launch (start us, length us, event | category | flops | bytes accessed | tf_op | source)
XLA Modules:
  0.0 119.4 jit_solution(4220783929235942311)
XLA Ops:
  1.9 3.0 %collective-permute-start.3 = (bf16[256,768]{1,0:T(8,128)(2,1)S(1)}, bf16[256,768]{1,0:T(8,128)(2,1)S(1)}, u32[]{:S(2)}, u32[]{:S(2)}) collective-permute-start(bf16[256,768]{1,0:T(8,128)(2,1)S(1)} %get-tuple-element.125), channel_id=1, source_target_pairs={{0,8},{8,0},{16,24},{24,16},{1,9},{9,1},{17,25},{25,17},{2,10},{10... | collective-permute-start | bytes 1179656 | tf_op jit(solution)/shard_map/ppermute | solution.py:270
  4.9 1.5 %collective-permute-start.6 = (bf16[256,768]{1,0:T(8,128)(2,1)S(1)}, bf16[256,768]{1,0:T(8,128)(2,1)S(1)}, u32[]{:S(2)}, u32[]{:S(2)}) collective-permute-start(bf16[256,768]{1,0:T(8,128)(2,1)S(1)} %get-tuple-element.124), channel_id=1, source_target_pairs={{0,16},{8,24},{16,0},{24,8},{1,17},{9,25},{17,1},{25,9},{2,18},{10... | collective-permute-start | bytes 1179656 | tf_op jit(solution)/shard_map/ppermute | solution.py:270
  6.5 1.9 %prep.1 = (bf16[272,768]{1,0:T(8,128)(2,1)S(1)}, bf16[256,256]{1,0:T(8,128)(2,1)S(1)}) custom-call(s32[2]{0:T(128)S(1)} %pad_add_fusion.pos_ref.core_ref, bf16[1024,768]{1,0:T(8,128)(2,1)} %land_ref.1, f32[4,1,256]{2,1,0:T(1,128)S(1)} %bitcast.4, bf16[1024,256]{1,0:T(8,128)(2,1)} %vec_ref.1), custom_call_target="tpu_custom_call" | custom-call | tf_op jit(solution)/shard_map/prep/pallas_call | solution.py:53
  9.2 5.7 %collective-permute-done.3.refs_0_ = bf16[256,768]{1,0:T(8,128)(2,1)S(1)} collective-permute-done((bf16[256,768]{1,0:T(8,128)(2,1)S(1)}, bf16[256,768]{1,0:T(8,128)(2,1)S(1)}, u32[]{:S(2)}, u32[]{:S(2)}) %collective-permute-start.3) | collective-permute-done | bytes 393248 | tf_op jit(solution)/shard_map/ppermute | solution.py:270
  14.9 3.1 %collective-permute-start.7 = (bf16[272,768]{1,0:T(8,128)(2,1)S(1)}, bf16[272,768]{1,0:T(8,128)(2,1)S(1)}, u32[]{:S(2)}, u32[]{:S(2)}) collective-permute-start(bf16[272,768]{1,0:T(8,128)(2,1)S(1)} %get-tuple-element.62.refs_1_.refs_4_.refs_2_), channel_id=1, source_target_pairs={{0,4},{1,5},{2,6},{3,7},{4,0},{5,1},{6,2},{7,3},{8,12},{9,13},{10,... | collective-permute-start | bytes 1253384 | tf_op jit(solution)/shard_map/ppermute | solution.py:270
  18.0 1.6 %collective-permute-start.1 = (bf16[272,768]{1,0:T(8,128)(2,1)S(1)}, bf16[272,768]{1,0:T(8,128)(2,1)S(1)}, u32[]{:S(2)}, u32[]{:S(2)}) collective-permute-start(bf16[272,768]{1,0:T(8,128)(2,1)S(1)} %get-tuple-element.62.refs_1_.refs_4_.refs_2_), channel_id=1, source_target_pairs={{0,2},{1,3},{2,0},{3,1},{4,6},{5,7},{6,4},{7,5},{8,10},{9,11},{10,... | collective-permute-start | bytes 1253384 | tf_op jit(solution)/shard_map/ppermute | solution.py:270
  25.4 10.4 %collective-permute-done.7.refs_1_.refs_4_.refs_2_ = bf16[272,768]{1,0:T(8,128)(2,1)S(1)} collective-permute-done((bf16[272,768]{1,0:T(8,128)(2,1)S(1)}, bf16[272,768]{1,0:T(8,128)(2,1)S(1)}, u32[]{:S(2)}, u32[]{:S(2)}) %collective-permute-start.7) | collective-permute-done | bytes 417824 | tf_op jit(solution)/shard_map/ppermute | solution.py:270
  37.7 1.5 %collective-permute-start.12 = (bf16[256,768]{1,0:T(8,128)(2,1)S(1)}, bf16[256,768]{1,0:T(8,128)(2,1)S(1)}, u32[]{:S(2)}, u32[]{:S(2)}) collective-permute-start(bf16[256,768]{1,0:T(8,128)(2,1)S(1)} %collective-permute-done.3.refs_0_), channel_id=1, source_target_pairs={{0,16},{8,24},{16,0},{24,8},{1,17},{9,25},{17,1},{25,9},{2,18},{10... | collective-permute-start | bytes 1179656 | tf_op jit(solution)/shard_map/ppermute | solution.py:270
  40.7 6.5 %collective-permute-done.10 = bf16[272,768]{1,0:T(8,128)(2,1)S(1)} collective-permute-done((bf16[272,768]{1,0:T(8,128)(2,1)S(1)}, bf16[272,768]{1,0:T(8,128)(2,1)S(1)}, u32[]{:S(2)}, u32[]{:S(2)}) %collective-permute-start.10) | collective-permute-done | bytes 417824 | tf_op jit(solution)/shard_map/ppermute | solution.py:309
  51.9 2.6 %collective-permute-start.17 = (bf16[256,256]{1,0:T(8,128)(2,1)S(1)}, bf16[256,256]{1,0:T(8,128)(2,1)S(1)}, u32[]{:S(2)}, u32[]{:S(2)}) collective-permute-start(bf16[256,256]{1,0:T(8,128)(2,1)S(1)} %get-tuple-element.93.refs_4_), channel_id=1, source_target_pairs={{0,4},{1,5},{2,6},{3,7},{4,0},{5,1},{6,2},{7,3},{8,12},{9,13},{10,... | collective-permute-start | bytes 393224 | tf_op jit(solution)/shard_map/ppermute | solution.py:270
  55.2 3.8 %collective-permute-start.15 = (bf16[256,256]{1,0:T(8,128)(2,1)S(1)}, bf16[256,256]{1,0:T(8,128)(2,1)S(1)}, u32[]{:S(2)}, u32[]{:S(2)}) collective-permute-start(bf16[256,256]{1,0:T(8,128)(2,1)S(1)} %get-tuple-element.93.refs_4_), channel_id=1, source_target_pairs={{0,2},{1,3},{2,0},{3,1},{4,6},{5,7},{6,4},{7,5},{8,10},{9,11},{10,... | collective-permute-start | bytes 393224 | tf_op jit(solution)/shard_map/ppermute | solution.py:270
  69.0 1.5 %collective-permute-start.23 = (f32[4,512]{1,0:T(4,128)S(1)}, f32[4,512]{1,0:T(4,128)S(1)}, u32[]{:S(2)}, u32[]{:S(2)}) collective-permute-start(f32[4,512]{1,0:T(4,128)S(1)} %maximum_add_fusion.refs_12_), channel_id=1, source_target_pairs={{0,2},{1,3},{2,0},{3,1},{4,6},{5,7},{6,4},{7,5},{8,10},{9,11},{10,... | collective-permute-start | bytes 24584 | tf_op jit(solution)/shard_map/ppermute | solution.py:270
  70.5 2.6 %collective-permute-start.24 = (f32[4,512]{1,0:T(4,128)S(1)}, f32[4,512]{1,0:T(4,128)S(1)}, u32[]{:S(2)}, u32[]{:S(2)}) collective-permute-start(f32[4,512]{1,0:T(4,128)S(1)} %maximum_add_fusion.refs_12_), channel_id=1, source_target_pairs={{0,4},{1,5},{2,6},{3,7},{4,0},{5,1},{6,2},{7,3},{8,12},{9,13},{10,... | collective-permute-start | bytes 24584 | tf_op jit(solution)/shard_map/ppermute | solution.py:270
  75.1 3.5 %collective-permute-done.25.refs_15_ = f32[4,512]{1,0:T(4,128)S(1)} collective-permute-done((f32[4,512]{1,0:T(4,128)S(1)}, f32[4,512]{1,0:T(4,128)S(1)}, u32[]{:S(2)}, u32[]{:S(2)}) %collective-permute-start.25) | collective-permute-done | bytes 8224 | tf_op jit(solution)/shard_map/ppermute | solution.py:270
  80.9 1.5 %collective-permute-start.26 = (bf16[528,256]{1,0:T(8,128)(2,1)S(1)}, bf16[528,256]{1,0:T(8,128)(2,1)S(1)}, u32[]{:S(2)}, u32[]{:S(2)}) collective-permute-start(bf16[528,256]{1,0:T(8,128)(2,1)S(1)} %shard_map.82), channel_id=1, source_target_pairs={{0,8},{8,0},{16,24},{24,16},{1,9},{9,1},{17,25},{25,17},{2,10},{10... | collective-permute-start | bytes 811016 | tf_op jit(solution)/shard_map/ppermute | solution.py:270
  82.4 1.5 %collective-permute-start.27 = (bf16[528,256]{1,0:T(8,128)(2,1)S(1)}, bf16[528,256]{1,0:T(8,128)(2,1)S(1)}, u32[]{:S(2)}, u32[]{:S(2)}) collective-permute-start(bf16[528,256]{1,0:T(8,128)(2,1)S(1)} %shard_map.81), channel_id=1, source_target_pairs={{0,16},{8,24},{16,0},{24,8},{1,17},{9,25},{17,1},{25,9},{2,18},{10... | collective-permute-start | bytes 811016 | tf_op jit(solution)/shard_map/ppermute | solution.py:270
  85.1 5.1 %collective-permute-done.26.refs_1_ = bf16[528,256]{1,0:T(8,128)(2,1)S(1)} collective-permute-done((bf16[528,256]{1,0:T(8,128)(2,1)S(1)}, bf16[528,256]{1,0:T(8,128)(2,1)S(1)}, u32[]{:S(2)}, u32[]{:S(2)}) %collective-permute-start.26) | collective-permute-done | bytes 270368 | tf_op jit(solution)/shard_map/ppermute | solution.py:270
  90.3 4.8 %collective-permute-done.27.refs_2_ = bf16[528,256]{1,0:T(8,128)(2,1)S(1)} collective-permute-done((bf16[528,256]{1,0:T(8,128)(2,1)S(1)}, bf16[528,256]{1,0:T(8,128)(2,1)S(1)}, u32[]{:S(2)}, u32[]{:S(2)}) %collective-permute-start.27) | collective-permute-done | bytes 270368 | tf_op jit(solution)/shard_map/ppermute | solution.py:270
  95.0 1.5 %finish.1 = (f32[512,256]{1,0:T(8,128)}, f32[128,256]{1,0:T(8,128)S(1)}, bf16[128,256]{1,0:T(8,128)(2,1)S(1)}) custom-call(s32[2]{0:T(128)S(1)} %pad_add_fusion.pos_ref.core_ref, f32[512,256]{1,0:T(8,128)S(1)} %shard_map.83.refs_0_, bf16[528,256]{1,0:T(8,128)(2,1)S(1)} %collective-permute-done.26.refs_1_, ...), custom_call_target="tpu_custom_call" | custom-call | tf_op jit(solution)/shard_map/finish/pallas_call | solution.py:234
  99.2 3.0 %collective-permute-done.30 = bf16[128,256]{1,0:T(8,128)(2,1)S(1)} collective-permute-done((bf16[128,256]{1,0:T(8,128)(2,1)S(1)}, bf16[128,256]{1,0:T(8,128)(2,1)S(1)}, u32[]{:S(2)}, u32[]{:S(2)}) %collective-permute-start.30) | collective-permute-done | bytes 65568 | tf_op jit(solution)/shard_map/ppermute | solution.py:270
  102.2 1.6 %collective-permute-start.31 = (bf16[128,256]{1,0:T(8,128)(2,1)S(1)}, bf16[128,256]{1,0:T(8,128)(2,1)S(1)}, u32[]{:S(2)}, u32[]{:S(2)}) collective-permute-start(bf16[128,256]{1,0:T(8,128)(2,1)S(1)} %get-tuple-element.122), channel_id=1, source_target_pairs={{0,16},{8,24},{16,0},{24,8},{1,17},{9,25},{17,1},{25,9},{2,18},{10... | collective-permute-start | bytes 196616 | tf_op jit(solution)/shard_map/ppermute | solution.py:270
  103.8 2.7 %collective-permute-done.31 = bf16[128,256]{1,0:T(8,128)(2,1)S(1)} collective-permute-done((bf16[128,256]{1,0:T(8,128)(2,1)S(1)}, bf16[128,256]{1,0:T(8,128)(2,1)S(1)}, u32[]{:S(2)}, u32[]{:S(2)}) %collective-permute-start.31) | collective-permute-done | bytes 65568 | tf_op jit(solution)/shard_map/ppermute | solution.py:270
  106.6 4.3 %collective-permute-done.32 = bf16[128,256]{1,0:T(8,128)(2,1)S(1)} collective-permute-done((bf16[128,256]{1,0:T(8,128)(2,1)S(1)}, bf16[128,256]{1,0:T(8,128)(2,1)S(1)}, u32[]{:S(2)}, u32[]{:S(2)}) %collective-permute-start.32) | collective-permute-done | bytes 65568 | tf_op jit(solution)/shard_map/ppermute | solution.py:270
  111.0 5.6 %collective-permute-done.33 = bf16[128,256]{1,0:T(8,128)(2,1)S(1)} collective-permute-done((bf16[128,256]{1,0:T(8,128)(2,1)S(1)}, bf16[128,256]{1,0:T(8,128)(2,1)S(1)}, u32[]{:S(2)}, u32[]{:S(2)}) %collective-permute-start.33) | collective-permute-done | bytes 65568 | tf_op jit(solution)/shard_map/ppermute | solution.py:270
  (84 shorter events, 37.3 us)
Async XLA Ops:
  1.9 13.0 %collective-permute-start.3 = (bf16[256,768]{1,0:T(8,128)(2,1)S(1)}, bf16[256,768]{1,0:T(8,128)(2,1)S(1)}, u32[]{:S(2)}, u32[]{:S(2)}) collective-permute-start(bf16[256,768]{1,0:T(8,128)(2,1)S(1)} %get-tuple-element.125), channel_id=1, source_target_pairs={{0,8},{8,0},{16,24},{24,16},{1,9},{9,1},{17,25},{25,17},{2,10},{10... | collective-permute-start | bytes 1179656 | tf_op jit(solution)/shard_map/ppermute | solution.py:270
  4.9 13.1 %collective-permute-start.6 = (bf16[256,768]{1,0:T(8,128)(2,1)S(1)}, bf16[256,768]{1,0:T(8,128)(2,1)S(1)}, u32[]{:S(2)}, u32[]{:S(2)}) collective-permute-start(bf16[256,768]{1,0:T(8,128)(2,1)S(1)} %get-tuple-element.124), channel_id=1, source_target_pairs={{0,16},{8,24},{16,0},{24,8},{1,17},{9,25},{17,1},{25,9},{2,18},{10... | collective-permute-start | bytes 1179656 | tf_op jit(solution)/shard_map/ppermute | solution.py:270
  8.4 11.2 %collective-permute-start = (bf16[272,768]{1,0:T(8,128)(2,1)S(1)}, bf16[272,768]{1,0:T(8,128)(2,1)S(1)}, u32[]{:S(2)}, u32[]{:S(2)}) collective-permute-start(bf16[272,768]{1,0:T(8,128)(2,1)S(1)} %get-tuple-element.62.refs_1_.refs_4_.refs_2_), channel_id=1, source_target_pairs={{0,1},{1,0},{2,3},{3,2},{4,5},{5,4},{6,7},{7,6},{8,9},{9,8},{10,11... | collective-permute-start | bytes 1253384 | tf_op jit(solution)/shard_map/ppermute | solution.py:270
  8.5 14.0 %collective-permute-start.4 = (bf16[256,768]{1,0:T(8,128)(2,1)S(1)}, bf16[256,768]{1,0:T(8,128)(2,1)S(1)}, u32[]{:S(2)}, u32[]{:S(2)}) collective-permute-start(bf16[256,768]{1,0:T(8,128)(2,1)S(1)} %get-tuple-element.124), channel_id=1, source_target_pairs={{0,8},{8,0},{16,24},{24,16},{1,9},{9,1},{17,25},{25,17},{2,10},{10... | collective-permute-start | bytes 1179656 | tf_op jit(solution)/shard_map/ppermute | solution.py:270
  9.1 14.8 %collective-permute-start.5 = (bf16[256,768]{1,0:T(8,128)(2,1)S(1)}, bf16[256,768]{1,0:T(8,128)(2,1)S(1)}, u32[]{:S(2)}, u32[]{:S(2)}) collective-permute-start(bf16[256,768]{1,0:T(8,128)(2,1)S(1)} %get-tuple-element.125), channel_id=1, source_target_pairs={{0,16},{8,24},{16,0},{24,8},{1,17},{9,25},{17,1},{25,9},{2,18},{10... | collective-permute-start | bytes 1179656 | tf_op jit(solution)/shard_map/ppermute | solution.py:270
  14.9 20.9 %collective-permute-start.7 = (bf16[272,768]{1,0:T(8,128)(2,1)S(1)}, bf16[272,768]{1,0:T(8,128)(2,1)S(1)}, u32[]{:S(2)}, u32[]{:S(2)}) collective-permute-start(bf16[272,768]{1,0:T(8,128)(2,1)S(1)} %get-tuple-element.62.refs_1_.refs_4_.refs_2_), channel_id=1, source_target_pairs={{0,4},{1,5},{2,6},{3,7},{4,0},{5,1},{6,2},{7,3},{8,12},{9,13},{10,... | collective-permute-start | bytes 1253384 | tf_op jit(solution)/shard_map/ppermute | solution.py:270
  18.0 19.2 %collective-permute-start.1 = (bf16[272,768]{1,0:T(8,128)(2,1)S(1)}, bf16[272,768]{1,0:T(8,128)(2,1)S(1)}, u32[]{:S(2)}, u32[]{:S(2)}) collective-permute-start(bf16[272,768]{1,0:T(8,128)(2,1)S(1)} %get-tuple-element.62.refs_1_.refs_4_.refs_2_), channel_id=1, source_target_pairs={{0,2},{1,3},{2,0},{3,1},{4,6},{5,7},{6,4},{7,5},{8,10},{9,11},{10,... | collective-permute-start | bytes 1253384 | tf_op jit(solution)/shard_map/ppermute | solution.py:270
  19.6 19.6 %collective-permute-start.9 = (bf16[272,768]{1,0:T(8,128)(2,1)S(1)}, bf16[272,768]{1,0:T(8,128)(2,1)S(1)}, u32[]{:S(2)}, u32[]{:S(2)}) collective-permute-start(bf16[272,768]{1,0:T(8,128)(2,1)S(1)} %get-tuple-element.62.refs_1_.refs_4_.refs_2_), channel_id=1, source_target_pairs={{2,4},{3,5},{4,2},{5,3},{10,12},{11,13},{12,10},{13,11},{18,20},{1... | collective-permute-start | bytes 1253384 | tf_op jit(solution)/shard_map/ppermute | solution.py:307
  35.8 11.4 %collective-permute-start.10 = (bf16[272,768]{1,0:T(8,128)(2,1)S(1)}, bf16[272,768]{1,0:T(8,128)(2,1)S(1)}, u32[]{:S(2)}, u32[]{:S(2)}) collective-permute-start(bf16[272,768]{1,0:T(8,128)(2,1)S(1)} %collective-permute-done.7.refs_1_.refs_4_.refs_2_), channel_id=1, source_target_pairs={{4,6},{5,7},{2,0},{3,1},{12,14},{13,15},{10,8},{11,9},{20,22},{21,... | collective-permute-start | bytes 1253384 | tf_op jit(solution)/shard_map/ppermute | solution.py:309
  37.1 10.3 %collective-permute-start.8 = (bf16[272,768]{1,0:T(8,128)(2,1)S(1)}, bf16[272,768]{1,0:T(8,128)(2,1)S(1)}, u32[]{:S(2)}, u32[]{:S(2)}) collective-permute-start(bf16[272,768]{1,0:T(8,128)(2,1)S(1)} %collective-permute-done.7.refs_1_.refs_4_.refs_2_), channel_id=1, source_target_pairs={{0,1},{1,0},{2,3},{3,2},{4,5},{5,4},{6,7},{7,6},{8,9},{9,8},{10,11... | collective-permute-start | bytes 1253384 | tf_op jit(solution)/shard_map/ppermute | solution.py:270
  37.2 12.4 %collective-permute-start.2 = (bf16[272,768]{1,0:T(8,128)(2,1)S(1)}, bf16[272,768]{1,0:T(8,128)(2,1)S(1)}, u32[]{:S(2)}, u32[]{:S(2)}) collective-permute-start(bf16[272,768]{1,0:T(8,128)(2,1)S(1)} %collective-permute-done.1.refs_1_.refs_4_.refs_2_), channel_id=1, source_target_pairs={{0,1},{1,0},{2,3},{3,2},{4,5},{5,4},{6,7},{7,6},{8,9},{9,8},{10,11... | collective-permute-start | bytes 1253384 | tf_op jit(solution)/shard_map/ppermute | solution.py:270
  37.7 17.5 %collective-permute-start.12 = (bf16[256,768]{1,0:T(8,128)(2,1)S(1)}, bf16[256,768]{1,0:T(8,128)(2,1)S(1)}, u32[]{:S(2)}, u32[]{:S(2)}) collective-permute-start(bf16[256,768]{1,0:T(8,128)(2,1)S(1)} %collective-permute-done.3.refs_0_), channel_id=1, source_target_pairs={{0,16},{8,24},{16,0},{24,8},{1,17},{9,25},{17,1},{25,9},{2,18},{10... | collective-permute-start | bytes 1179656 | tf_op jit(solution)/shard_map/ppermute | solution.py:270
  39.2 19.7 %collective-permute-start.13 = (bf16[256,768]{1,0:T(8,128)(2,1)S(1)}, bf16[256,768]{1,0:T(8,128)(2,1)S(1)}, u32[]{:S(2)}, u32[]{:S(2)}) collective-permute-start(bf16[256,768]{1,0:T(8,128)(2,1)S(1)} %collective-permute-done.6.refs_3_), channel_id=1, source_target_pairs={{0,8},{8,0},{16,24},{24,16},{1,9},{9,1},{17,25},{25,17},{2,10},{10... | collective-permute-start | bytes 1179656 | tf_op jit(solution)/shard_map/ppermute | solution.py:270
  47.3 16.2 %collective-permute-start.11 = (bf16[272,768]{1,0:T(8,128)(2,1)S(1)}, bf16[272,768]{1,0:T(8,128)(2,1)S(1)}, u32[]{:S(2)}, u32[]{:S(2)}) collective-permute-start(bf16[272,768]{1,0:T(8,128)(2,1)S(1)} %add.24.refs_1_.refs_4_.refs_2_), channel_id=1, source_target_pairs={{0,1},{1,0},{2,3},{3,2},{4,5},{5,4},{6,7},{7,6},{8,9},{9,8},{10,11... | collective-permute-start | bytes 1253384 | tf_op jit(solution)/shard_map/ppermute | solution.py:270
  51.9 10.1 %collective-permute-start.17 = (bf16[256,256]{1,0:T(8,128)(2,1)S(1)}, bf16[256,256]{1,0:T(8,128)(2,1)S(1)}, u32[]{:S(2)}, u32[]{:S(2)}) collective-permute-start(bf16[256,256]{1,0:T(8,128)(2,1)S(1)} %get-tuple-element.93.refs_4_), channel_id=1, source_target_pairs={{0,4},{1,5},{2,6},{3,7},{4,0},{5,1},{6,2},{7,3},{8,12},{9,13},{10,... | collective-permute-start | bytes 393224 | tf_op jit(solution)/shard_map/ppermute | solution.py:270
  54.5 12.6 %collective-permute-start.19 = (bf16[256,256]{1,0:T(8,128)(2,1)S(1)}, bf16[256,256]{1,0:T(8,128)(2,1)S(1)}, u32[]{:S(2)}, u32[]{:S(2)}) collective-permute-start(bf16[256,256]{1,0:T(8,128)(2,1)S(1)} %get-tuple-element.93.refs_4_), channel_id=1, source_target_pairs={{2,4},{3,5},{4,2},{5,3},{10,12},{11,13},{12,10},{13,11},{18,20},{1... | collective-permute-start | bytes 393224 | tf_op jit(solution)/shard_map/ppermute | solution.py:307
  55.2 12.0 %collective-permute-start.15 = (bf16[256,256]{1,0:T(8,128)(2,1)S(1)}, bf16[256,256]{1,0:T(8,128)(2,1)S(1)}, u32[]{:S(2)}, u32[]{:S(2)}) collective-permute-start(bf16[256,256]{1,0:T(8,128)(2,1)S(1)} %get-tuple-element.93.refs_4_), channel_id=1, source_target_pairs={{0,2},{1,3},{2,0},{3,1},{4,6},{5,7},{6,4},{7,5},{8,10},{9,11},{10,... | collective-permute-start | bytes 393224 | tf_op jit(solution)/shard_map/ppermute | solution.py:270
  62.0 6.8 %collective-permute-start.20 = (bf16[256,256]{1,0:T(8,128)(2,1)S(1)}, bf16[256,256]{1,0:T(8,128)(2,1)S(1)}, u32[]{:S(2)}, u32[]{:S(2)}) collective-permute-start(bf16[256,256]{1,0:T(8,128)(2,1)S(1)} %collective-permute-done.17.refs_8_), channel_id=1, source_target_pairs={{4,6},{5,7},{2,0},{3,1},{12,14},{13,15},{10,8},{11,9},{20,22},{21,... | collective-permute-start | bytes 393224 | tf_op jit(solution)/shard_map/ppermute | solution.py:309
  67.1 6.6 %collective-permute-start.18 = (bf16[256,256]{1,0:T(8,128)(2,1)S(1)}, bf16[256,256]{1,0:T(8,128)(2,1)S(1)}, u32[]{:S(2)}, u32[]{:S(2)}) collective-permute-start(bf16[256,256]{1,0:T(8,128)(2,1)S(1)} %collective-permute-done.17.refs_8_), channel_id=1, source_target_pairs={{0,1},{1,0},{2,3},{3,2},{4,5},{5,4},{6,7},{7,6},{8,9},{9,8},{10,11... | collective-permute-start | bytes 393224 | tf_op jit(solution)/shard_map/ppermute | solution.py:270
  67.2 6.0 %collective-permute-start.16 = (bf16[256,256]{1,0:T(8,128)(2,1)S(1)}, bf16[256,256]{1,0:T(8,128)(2,1)S(1)}, u32[]{:S(2)}, u32[]{:S(2)}) collective-permute-start(bf16[256,256]{1,0:T(8,128)(2,1)S(1)} %collective-permute-done.15.refs_6_), channel_id=1, source_target_pairs={{0,1},{1,0},{2,3},{3,2},{4,5},{5,4},{6,7},{7,6},{8,9},{9,8},{10,11... | collective-permute-start | bytes 393224 | tf_op jit(solution)/shard_map/ppermute | solution.py:270
  80.9 9.4 %collective-permute-start.26 = (bf16[528,256]{1,0:T(8,128)(2,1)S(1)}, bf16[528,256]{1,0:T(8,128)(2,1)S(1)}, u32[]{:S(2)}, u32[]{:S(2)}) collective-permute-start(bf16[528,256]{1,0:T(8,128)(2,1)S(1)} %shard_map.82), channel_id=1, source_target_pairs={{0,8},{8,0},{16,24},{24,16},{1,9},{9,1},{17,25},{25,17},{2,10},{10... | collective-permute-start | bytes 811016 | tf_op jit(solution)/shard_map/ppermute | solution.py:270
  82.4 12.7 %collective-permute-start.27 = (bf16[528,256]{1,0:T(8,128)(2,1)S(1)}, bf16[528,256]{1,0:T(8,128)(2,1)S(1)}, u32[]{:S(2)}, u32[]{:S(2)}) collective-permute-start(bf16[528,256]{1,0:T(8,128)(2,1)S(1)} %shard_map.81), channel_id=1, source_target_pairs={{0,16},{8,24},{16,0},{24,8},{1,17},{9,25},{17,1},{25,9},{2,18},{10... | collective-permute-start | bytes 811016 | tf_op jit(solution)/shard_map/ppermute | solution.py:270
  83.9 11.2 %collective-permute-start.28 = (bf16[528,256]{1,0:T(8,128)(2,1)S(1)}, bf16[528,256]{1,0:T(8,128)(2,1)S(1)}, u32[]{:S(2)}, u32[]{:S(2)}) collective-permute-start(bf16[528,256]{1,0:T(8,128)(2,1)S(1)} %shard_map.80), channel_id=1, source_target_pairs={{0,24},{8,16},{16,8},{24,0},{1,25},{9,17},{17,9},{25,1},{2,26},{10... | collective-permute-start | bytes 811016 | tf_op jit(solution)/shard_map/ppermute | solution.py:270
  110.9 5.7 %collective-permute-start.33 = (bf16[128,256]{1,0:T(8,128)(2,1)S(1)}, bf16[128,256]{1,0:T(8,128)(2,1)S(1)}, u32[]{:S(2)}, u32[]{:S(2)}) collective-permute-start(bf16[128,256]{1,0:T(8,128)(2,1)S(1)} %fusion.2), channel_id=1, source_target_pairs={{0,4},{1,5},{2,6},{3,7},{4,0},{5,1},{6,2},{7,3},{8,12},{9,13},{10,... | collective-permute-start | bytes 196616 | tf_op jit(solution)/shard_map/ppermute | solution.py:270
  (14 other events, 77.7 us)
